TPU v7x, 32 devices: a whole 2x2x4 slice. The times are simulated.
32 devices in a mesh: parts: 2 (over y), modes: 16 (over z, x, core).
Axes of the slice: x: 2, y: 2, z: 4, core: 2. Of those that a mesh axis runs over, the one named last changes fastest.
Arguments:
- stem: bfloat16 [2, 16, 64, 32, 512], P(None, 'modes', None, None, 'parts'), parts along dimension 4, may hold values from -6 to 6
- branch_one: bfloat16 [2, 1024, 1024], replicated, may hold values from -0.125 to 0.125
- branch_two: bfloat16 [2, 1024, 1024], replicated, may hold values from -0.125 to 0.125
- branch_three: bfloat16 [2, 2, 16, 512, 512], P(None, None, 'modes'), may hold values from -0.0625 to 0.0625
- leg_orders: int32 [2, 10], replicated, may hold values from 0 to 9, each once within a row
- slice_pick: int32 [32], P('parts'), parts along dimension 0, may hold values from 0 to 1
Outputs:
- contracted: bfloat16 [1024, 2, 2, 2, 256], P(('parts', 'modes')), parts along dimension 0
There are 2 independent parts, one for each index of `parts`. A program takes and returns all parts, laid end to end along the dimension named above; an argument that names none is the same for every part. Nothing has to cross between parts.
Inputs may be any that keep to these rules, and one draw needn't show every extreme that they name: `leg_orders`: each row names every input leg bit once.
All inputs are finite; a program needn't handle non-finite values.
Results may differ from a plain program's by a relative error of at most 0.008.
Values may be sent and summed in bfloat16 or wider, within the bound.
No kernel may reach another device: no remote copies, remote signals or barrier semaphores. Data moves between devices by JAX's collectives and lax.ppermute only.
A program may use at most 128 MiB of HBM per device.

v0:
```python
import jax
import jax.numpy as jnp
from jax import lax
from jax.experimental import pallas as pl
from jax.experimental.pallas import tpu as pltpu
from jax.sharding import PartitionSpec as P

BF = jnp.bfloat16
F32 = jnp.float32


def dot(lhs, rhs):
    return jnp.dot(lhs, rhs, preferred_element_type=F32)


def one_hot(orders_ref, row, start, width, leg_width):
    legs = leg_width.bit_length() - 1
    index = lax.broadcasted_iota(jnp.int32, (1, width), 1) + start
    placed = jnp.zeros((1, width), jnp.int32)
    for bit in range(legs):
        placed += jnp.left_shift(jnp.right_shift(index, bit) & 1, orders_ref[row, bit])
    rows = lax.broadcasted_iota(jnp.int32, (leg_width, width), 0)
    return jnp.where(rows == placed, 1.0, 0.0).astype(BF)


def turn_kernel(half_ref, orders_ref, one_ref, two_ref, out_one_ref, out_two_ref, pick_one, pick_two):
    leg_width = one_ref.shape[2]
    width = leg_width // 2

    @pl.when((pl.program_id(0) == 0) & (pl.program_id(1) == 0))
    def _():
        pick_one[...] = one_hot(orders_ref, 0, half_ref[0] * width, width, leg_width)
        pick_two[...] = one_hot(orders_ref, 1, 0, leg_width, leg_width)

    out_one_ref[0] = dot(one_ref[0], pick_one[...]).astype(BF)
    out_two_ref[0] = dot(two_ref[0], pick_two[...]).astype(BF)


def turned(half, orders, one, two):
    leg_width = one.shape[2]
    width = leg_width // 2
    rows = 256
    spec = lambda wide: pl.BlockSpec((1, rows, wide), lambda r, i, *_: (r, i, 0))
    return pl.pallas_call(
        turn_kernel,
        grid_spec=pltpu.PrefetchScalarGridSpec(
            num_scalar_prefetch=2,
            grid=(2, leg_width // rows),
            in_specs=[spec(leg_width), spec(leg_width)],
            out_specs=[spec(width), spec(leg_width)],
            scratch_shapes=[pltpu.VMEM((leg_width, width), BF), pltpu.VMEM((leg_width, leg_width), BF)],
        ),
        out_shape=[
            jax.ShapeDtypeStruct((2, leg_width, width), BF),
            jax.ShapeDtypeStruct((2, leg_width, leg_width), BF),
        ],
        name="turn",
    )(half, orders, one, two)


def complex_dot(wr, wi, vr, vi):
    return dot(wr, vr) - dot(wi, vi), dot(wr, vi) + dot(wi, vr)


def chain_kernel(x_ref, one_ref, two_ref, out_ref, first):
    half = one_ref.shape[1] // 2
    lanes = x_ref.shape[5]
    inner = x_ref.shape[0] * x_ref.shape[4]

    def step_one(n, _):
        a, d, t = n >> 2, (n >> 1) & 1, n & 1
        rows = pl.ds(pl.multiple_of(t * half, half), half)
        vr = x_ref[:, 0, a, d].reshape(inner, lanes)
        vi = x_ref[:, 1, a, d].reshape(inner, lanes)
        yr, yi = complex_dot(one_ref[0, rows, :], one_ref[1, rows, :], vr, vi)
        first[a, t, d, 0] = yr.astype(BF)
        first[a, t, d, 1] = yi.astype(BF)
        return 0

    lax.fori_loop(0, 8, step_one, 0)

    def step_two(n, _):
        t, d, u = n >> 2, (n >> 1) & 1, n & 1
        rows = pl.ds(pl.multiple_of(u * half, half), half)
        vr = first[:, t, d, 0].reshape(2 * half, lanes)
        vi = first[:, t, d, 1].reshape(2 * half, lanes)
        yr, yi = complex_dot(two_ref[0, rows, :], two_ref[1, rows, :], vr, vi)
        out_ref[t, d, 0, u] = yr.astype(BF)
        out_ref[t, d, 1, u] = yi.astype(BF)
        return 0

    lax.fori_loop(0, 8, step_two, 0)


def chained(x, one, two):
    half = one.shape[1] // 2
    lanes = x.shape[5]
    return pl.pallas_call(
        chain_kernel,
        out_shape=jax.ShapeDtypeStruct((2, 2, 2, 2, half, lanes), BF),
        scratch_shapes=[pltpu.VMEM((2, 2, 2, 2, half, lanes), BF)],
        name="chain",
    )(x, one, two)


def join_kernel(place_ref, w0, w1, w2, w3, v_ref, out_ref):
    lanes = v_ref.shape[5]
    t0, d0 = place_ref[0], place_ref[1]
    spots = ((t0, d0), (1 - t0, d0), (t0, 1 - d0), (1 - t0, 1 - d0))
    weights = (w0, w1, w2, w3)
    wr = jnp.concatenate([w[0] for w in weights], axis=1)
    wi = jnp.concatenate([w[1] for w in weights], axis=1)
    for u in range(2):
        vr = jnp.concatenate([v_ref[t, d, 0, u] for t, d in spots], axis=0)
        vi = jnp.concatenate([v_ref[t, d, 1, u] for t, d in spots], axis=0)
        yr, yi = complex_dot(wr, wi, vr, vi)
        out_ref[:, u * lanes:(u + 1) * lanes] = yr.astype(BF)
        out_ref[:, (2 + u) * lanes:(3 + u) * lanes] = yi.astype(BF)


def joined(place, weights, v):
    smem = pl.BlockSpec(memory_space=pltpu.SMEM)
    vmem = pl.BlockSpec(memory_space=pltpu.VMEM)
    return pl.pallas_call(
        join_kernel,
        in_specs=[smem] + [vmem] * 5,
        out_shape=jax.ShapeDtypeStruct((weights[0].shape[1], 4 * v.shape[5]), BF),
        name="join",
    )(place, *weights, v)


def per_device(stem, branch_one, branch_two, branch_three, leg_orders, slice_pick):
    groups = lax.axis_size("modes")
    own = lax.axis_index("modes")
    side = groups // 2
    extent = stem.shape[2]
    lanes = stem.shape[4]
    top = own // side
    core = own % 2

    pieces = stem.reshape(2, extent, 2, side, 2, lanes).transpose(3, 0, 2, 4, 1, 5)
    halves = [list(range(side)), list(range(side, groups))]
    arrived = lax.all_to_all(pieces, "modes", 0, 0, tiled=True, axis_index_groups=halves)
    if extent % 16:
        arrived = arrived.transpose(1, 2, 3, 0, 4, 5).reshape(1, 2, 2, 2, side * extent, lanes)

    own_pick = lax.dynamic_index_in_dim(slice_pick, own, 0, keepdims=False)
    chosen = lax.dynamic_index_in_dim(branch_three, own_pick, 0, keepdims=False)[:, 0]
    across = [(i, i ^ side) for i in range(groups)]
    beside = [(i, i ^ 1) for i in range(groups)]
    other = lax.ppermute(chosen, "modes", across)
    chosen_beside = lax.ppermute(chosen, "modes", beside)
    other_beside = lax.ppermute(other, "modes", beside)

    one, two = turned(top.reshape(1).astype(jnp.int32), leg_orders, branch_one, branch_two)
    v = chained(arrived, one, two)
    place = jnp.stack([top, core]).astype(jnp.int32)
    partial = joined(place, (chosen, other, chosen_beside, other_beside), v)

    out_width = partial.shape[0]
    share = out_width // groups
    spread = lax.all_to_all(partial.reshape(groups, share, 4 * lanes), "modes", 0, 0, tiled=True)
    spread = spread.reshape(side, 2, share, 2, 2, lanes).astype(F32)
    return jnp.sum(spread, axis=0).astype(BF).transpose(1, 2, 3, 0, 4)


def solution(mesh):
    in_specs = (
        P(None, "modes", None, None, "parts"),
        P(),
        P(),
        P(None, None, "modes", None, None),
        P(),
        P("parts"),
    )
    out_specs = P(("parts", "modes"), None, None, None, None)
    return jax.shard_map(
        per_device, mesh=mesh, in_specs=in_specs, out_specs=out_specs, check_vma=False
    )
```

profile of v0, /device:TPU:1, one launch (start us, length us, event | category | flops | bytes accessed | tf_op | source)
XLA Modules:
  0.0 140.7 jit_solution(14897292912210274275)
XLA Ops:
  0.0 0.0 copy-start
  0.0 2.9 %copy.9 = bf16[2,1,64,32,256]{4,2,3,0,1:T(8,128)(2,1)S(1)} copy(bf16[2,1,64,32,256]{4,3,2,1,0:T(8,128)(2,1)} %param.6) | data formatting | bytes 4194304 | tf_op args[0]
  2.9 1.5 %copy.13 = bf16[2,64,2,8,2,256]{5,1,4,2,0,3:T(8,128)(2,1)} copy(bf16[2,64,2,8,2,256]{5,1,4,3,2,0:T(8,128)(2,1)S(1)} %bitcast.12) | data formatting | bytes 4194304 | tf_op jit(solution)/shard_map/reshape | solution.py:141
  4.4 5.4 %all-to-all-start = ((bf16[8,2,2,2,64,256]{5,4,3,2,1,0:T(8,128)(2,1)}), bf16[8,2,2,2,64,256]{5,4,3,2,1,0:T(8,128)(2,1)}, u32[]{:S(2)}, u32[]{:S(2)}) async-start(bf16[8,2,2,2,64,256]{5,4,3,2,1,0:T(8,128)(2,1)} %bitcast.11), calls=%async_computation | async-start | bytes 4194304 | tf_op jit(solution)/shard_map/all_to_all | solution.py:143
  9.8 0.0 copy-done.2
  9.8 0.6 dynamic_slice.8
  12.3 0.0 copy-done
  12.4 0.1 dynamic-slice_bitcast_fusion.w0
  12.4 0.0 copy-start.1
  12.4 2.8 %collective-permute-start = (bf16[2,512,512]{2,1,0:T(8,128)(2,1)S(1)}, bf16[2,512,512]{2,1,0:T(8,128)(2,1)}, u32[]{:S(2)}, u32[]{:S(2)}) collective-permute-start(bf16[2,512,512]{2,1,0:T(8,128)(2,1)S(1)} %dynamic-slice_bitcast_fusion.w0), channel_id=1, source_target_pairs={{0,8},{1,9},{2,10},{3,11},{4,12},{5,13},{6,14},{7,15},{8,0},{9,1},... | collective-permute-start | bytes 3145736 | tf_op jit(solution)/shard_map/ppermute | solution.py:151
  15.3 0.4 collective-permute-start.1
  15.7 45.6 %collective-permute-done.w1 = bf16[2,512,512]{2,1,0:T(8,128)(2,1)} collective-permute-done((bf16[2,512,512]{2,1,0:T(8,128)(2,1)S(1)}, bf16[2,512,512]{2,1,0:T(8,128)(2,1)}, u32[]{:S(2)}, u32[]{:S(2)}) %collective-permute-start) | collective-permute-done | bytes 1048608 | tf_op jit(solution)/shard_map/ppermute | solution.py:151
  61.3 0.7 collective-permute-start.2
  62.0 12.8 %turn.1 = (bf16[2,1024,512]{2,1,0:T(8,128)(2,1)}, bf16[2,1024,1024]{2,1,0:T(8,128)(2,1)}) custom-call(s32[1]{0:T(128)} %bitcast.half_ref, s32[2,10]{1,0:T(2,128)} %orders_ref.1, bf16[2,1024,1024]{2,1,0:T(8,128)(2,1)} %one_ref.1, bf16[2,1024,1024]{2,1,0:T(8,128)(2,1)} %two_ref.1), custom_call_target="tpu_custom_call" | custom-call | tf_op jit(solution)/shard_map/turn/pallas_call | solution.py:44
  74.8 0.6 pad_add_fusion.place_ref
  75.4 0.0 all-to-all-done.x_ref
  75.4 21.1 %chain.1.v_ref = bf16[2,2,2,2,512,256]{5,4,3,2,1,0:T(8,128)(2,1)} custom-call(bf16[8,2,2,2,64,256]{5,4,3,2,1,0:T(8,128)(2,1)} %all-to-all-done.x_ref, bf16[2,1024,512]{2,1,0:T(8,128)(2,1)} %get-tuple-element.7.one_ref, bf16[2,1024,1024]{2,1,0:T(8,128)(2,1)} %get-tuple-element.8.two_ref), custom_call_target="tpu_custom_call" | custom-call | tf_op jit(solution)/shard_map/chain/pallas_call | solution.py:98
  96.5 0.0 collective-permute-done.1.w2
  96.5 0.0 collective-permute-done.2.w3
  96.5 9.0 %join.1 = bf16[512,1024]{1,0:T(8,128)(2,1)} custom-call(s32[2]{0:T(128)} %pad_add_fusion.place_ref, bf16[2,512,512]{2,1,0:T(8,128)(2,1)} %copy-done.1, bf16[2,512,512]{2,1,0:T(8,128)(2,1)} %collective-permute-done.w1, bf16[2,512,512]{2,1,0:T(8,128)(2,1)} %collective-permute-done.1.w2, bf16[2,512,512]{2,1,0:T(8,128)(2,1)} %collective-permute-done.2.w3, ...), custom_call_target="tpu_custom_call" | custom-call | tf_op jit(solution)/shard_map/join/pallas_call | solution.py:124
  105.4 31.4 %all_to_all.10 = bf16[16,32,1024]{2,1,0:T(8,128)(2,1)} all-to-all(bf16[16,32,1024]{2,1,0:T(8,128)(2,1)} %bitcast.13), channel_id=1, replica_groups=mesh['parts'=2,'modes'=16] {'modes'}, dimensions={0} | all-to-all | bytes 2097152 | tf_op jit(solution)/shard_map/all_to_all | solution.py:162
  136.8 1.8 %reshape.13 = bf16[8,2,32,2,2,256]{5,4,3,2,1,0:T(2,128)(2,1)S(1)} reshape(bf16[16,32,1024]{2,1,0:T(8,128)(2,1)} %all_to_all.10) | data formatting | bytes 2097152 | tf_op jit(solution)/shard_map/reshape | solution.py:163
  138.7 1.2 reduce_sum.12
  139.9 0.8 copy.11
  (2 shorter events, 0.0 us)
Async XLA Ops:
  0.0 12.3 %copy-start = (bf16[2,2,1,512,512]{4,3,2,1,0:T(8,128)(2,1)S(1)}, bf16[2,2,1,512,512]{4,3,2,1,0:T(8,128)(2,1)}, u32[]{:S(2)}) copy-start(bf16[2,2,1,512,512]{4,3,2,1,0:T(8,128)(2,1)} %param.9) | copy-start | bytes 6291460
  4.4 5.4 %copy-start.2 = (s32[16]{0:T(128)S(1)}, s32[16]{0:T(128)}, u32[]{:S(2)}) copy-start(s32[16]{0:T(128)} %param.11) | copy-start | bytes 196
  4.4 71.0 %all-to-all-start = ((bf16[8,2,2,2,64,256]{5,4,3,2,1,0:T(8,128)(2,1)}), bf16[8,2,2,2,64,256]{5,4,3,2,1,0:T(8,128)(2,1)}, u32[]{:S(2)}, u32[]{:S(2)}) async-start(bf16[8,2,2,2,64,256]{5,4,3,2,1,0:T(8,128)(2,1)} %bitcast.11), calls=%async_computation | async-start | bytes 4194304 | tf_op jit(solution)/shard_map/all_to_all | solution.py:143
  12.4 62.4 %copy-start.1 = (bf16[2,512,512]{2,1,0:T(8,128)(2,1)}, bf16[2,512,512]{2,1,0:T(8,128)(2,1)S(1)}, u32[]{:S(2)}) copy-start(bf16[2,512,512]{2,1,0:T(8,128)(2,1)S(1)} %dynamic-slice_bitcast_fusion.w0) | copy-start | bytes 3145732
  12.4 48.9 %collective-permute-start = (bf16[2,512,512]{2,1,0:T(8,128)(2,1)S(1)}, bf16[2,512,512]{2,1,0:T(8,128)(2,1)}, u32[]{:S(2)}, u32[]{:S(2)}) collective-permute-start(bf16[2,512,512]{2,1,0:T(8,128)(2,1)S(1)} %dynamic-slice_bitcast_fusion.w0), channel_id=1, source_target_pairs={{0,8},{1,9},{2,10},{3,11},{4,12},{5,13},{6,14},{7,15},{8,0},{9,1},... | collective-permute-start | bytes 3145736 | tf_op jit(solution)/shard_map/ppermute | solution.py:151
  15.3 81.2 %collective-permute-start.1 = (bf16[2,512,512]{2,1,0:T(8,128)(2,1)S(1)}, bf16[2,512,512]{2,1,0:T(8,128)(2,1)}, u32[]{:S(2)}, u32[]{:S(2)}) collective-permute-start(bf16[2,512,512]{2,1,0:T(8,128)(2,1)S(1)} %dynamic-slice_bitcast_fusion.w0), channel_id=1, source_target_pairs={{0,1},{1,0},{2,3},{3,2},{4,5},{5,4},{6,7},{7,6},{8,9},{9,8},{10,11... | collective-permute-start | bytes 3145736 | tf_op jit(solution)/shard_map/ppermute | solution.py:152
  61.3 35.2 %collective-permute-start.2 = (bf16[2,512,512]{2,1,0:T(8,128)(2,1)}, bf16[2,512,512]{2,1,0:T(8,128)(2,1)}, u32[]{:S(2)}, u32[]{:S(2)}) collective-permute-start(bf16[2,512,512]{2,1,0:T(8,128)(2,1)} %collective-permute-done.w1), channel_id=1, source_target_pairs={{0,1},{1,0},{2,3},{3,2},{4,5},{5,4},{6,7},{7,6},{8,9},{9,8},{10,11... | collective-permute-start | bytes 3145736 | tf_op jit(solution)/shard_map/ppermute | solution.py:153
where the time goes:
time: 141 us
  waiting for transfers between devices  45.6 us (32%)
  Pallas kernels  42.8 us (30%)
  blocking collectives  31.4 us (22%)
  starting transfers between devices  9.4 us (7%)
  local copies, waits for them, and re-layouts  7.7 us (5%)
  between operations  1.99 us (1%)
  other arithmetic  1.78 us (1%)
    ppermute x1, waiting for transfers between devices, per_device(): other = lax.ppermute(chosen, 'modes', across)  45.6 us
    all_to_all x1, blocking collectives, per_device(): lax.all_to_all(partial.reshape(groups, share, 4 * lanes), 'modes', 0, 0,...  31.4 us
    pallas_call x1, Pallas kernels, chained(): pl.pallas_call(chain_kernel, out_shape=jax.ShapeDtypeStruct((2, 2, 2, 2,...  21.1 us
    pallas_call x1, Pallas kernels, turned(): pl.pallas_call(turn_kernel, grid_spec=pltpu.PrefetchScalarGridSpec(num_sc...  12.8 us
    pallas_call x1, Pallas kernels, joined(): pl.pallas_call(join_kernel, in_specs=[smem] + [vmem] * 5, out_shape=jax.S...  8.95 us
    all_to_all x1, starting transfers between devices, per_device(): lax.all_to_all(pieces, 'modes', 0, 0, tiled=True, axis_index_groups=halves)  5.4 us
    unnamed x7, local copies, waits for them, and re-layouts  2.93 us
    ppermute x1, starting transfers between devices, per_device(): other = lax.ppermute(chosen, 'modes', across)  2.84 us
  transfers between devices with their start and end apart: 4, of which 1 were waited for; matrix products, arithmetic and copies ran while one was open for 1% of the time, Pallas kernels for 24%

commit v1 on v0

v1 whole, which is shorter than its diff:
```python
import jax
import jax.numpy as jnp
from jax import lax
from jax.experimental import pallas as pl
from jax.experimental.pallas import tpu as pltpu
from jax.sharding import PartitionSpec as P


BF = jnp.bfloat16
F32 = jnp.float32


def dot(lhs, rhs):
    return jnp.dot(lhs, rhs, preferred_element_type=F32)


def copies(sem, *pairs):
    return [pltpu.make_async_copy(src, dst, sem.at[n]) for n, (src, dst) in enumerate(pairs)]


def anywhere(count):
    return [pl.BlockSpec(memory_space=pl.ANY) for _ in range(count)]


def complex_dot(wr, wi, vr, vi):
    return dot(wr, vr) - dot(wi, vi), dot(wr, vi) + dot(wi, vr)


def turn_kernel(row, start_ref, orders_ref, branch_hbm, out_hbm, branch, out, pick, sem, out_sem):
    leg_width, width = pick.shape
    half = leg_width // 2
    pieces = [(r, pl.ds(u * half, half)) for r in range(2) for u in range(2)]
    loads = copies(sem, *[(branch_hbm.at[r, rows], branch.at[r, rows]) for r, rows in pieces])
    stores = copies(out_sem, *[(out.at[r, rows], out_hbm.at[r, rows]) for r, rows in pieces])
    for load in loads:
        load.start()

    index = lax.broadcasted_iota(jnp.int32, (1, width), 1) + start_ref[0]
    placed = jnp.zeros((1, width), jnp.int32)
    for bit in range(leg_width.bit_length() - 1):
        placed += jnp.left_shift(jnp.right_shift(index, bit) & 1, orders_ref[row, bit])
    ahead = placed - lax.broadcasted_iota(jnp.int32, (16, width), 0)

    def build(n, _):
        base = pl.multiple_of(n * 16, 16)
        pick[pl.ds(base, 16), :] = jnp.where(ahead == base, 1.0, 0.0).astype(BF)
        return 0

    lax.fori_loop(0, leg_width // 16, build, 0)
    for (r, rows), load, store in zip(pieces, loads, stores):
        load.wait()
        out[r, rows, :] = dot(branch[r, rows, :], pick[...]).astype(BF)
        store.start()
    for store in stores:
        store.wait()


def turned(row, start, width, orders, branch):
    leg_width = branch.shape[2]
    smem = pl.BlockSpec(memory_space=pltpu.SMEM)
    return pl.pallas_call(
        lambda *refs: turn_kernel(row, *refs),
        in_specs=[smem, smem] + anywhere(1),
        out_specs=anywhere(1)[0],
        out_shape=jax.ShapeDtypeStruct((2, leg_width, width), BF),
        scratch_shapes=[
            pltpu.VMEM(branch.shape, BF),
            pltpu.VMEM((2, leg_width, width), BF),
            pltpu.VMEM((leg_width, width), BF),
            pltpu.SemaphoreType.DMA((4,)),
            pltpu.SemaphoreType.DMA((4,)),
        ],
        cost_estimate=pl.CostEstimate(flops=4 * width * leg_width**2, transcendentals=0, bytes_accessed=4 * leg_width**2),
        name="turn",
    )(start, orders, branch)


def chain_kernel(place_ref, x_hbm, one_hbm, two_hbm, *refs):
    held_hbm, (v_hbm, part_hbm) = refs[:2], refs[2:4]
    x, one, two, held, first, v, part, x_sem, one_sem, two_sem, held_sem, v_sem, part_sem = refs[4:]
    half = one.shape[1] // 2
    lanes = x.shape[5]
    inner = x.shape[2] * x.shape[4]
    halves = [pl.ds(u * half, half) for u in range(2)]
    t0, d0 = place_ref[0], place_ref[1]
    spots = [(d, a) for d in range(2) for a in range(2)]
    x_loads = copies(x_sem, *[(x_hbm.at[:, :, a, d], x.at[d, a]) for d, a in spots])
    one_loads = copies(one_sem, *[(one_hbm.at[:, rows], one.at[:, rows]) for rows in halves])
    two_loads = copies(two_sem, *[(two_hbm.at[:, rows], two.at[:, rows]) for rows in halves])
    held_loads = copies(held_sem, *[(held_hbm[n], held.at[:, :, pl.ds(n * half, half)]) for n in range(2)])
    x_loads[0].start()
    one_loads[0].start()
    for load in x_loads[1:] + one_loads[1:] + two_loads + held_loads:
        load.start()

    for t in range(2):
        one_loads[t].wait()
        for d, a in spots:
            if t == 0:
                x_loads[2 * d + a].wait()
            vr = x[d, a, :, 0].reshape(inner, lanes)
            vi = x[d, a, :, 1].reshape(inner, lanes)
            yr, yi = complex_dot(one[0, halves[t], :], one[1, halves[t], :], vr, vi)
            first[d, a, t, 0] = yr.astype(BF)
            first[d, a, t, 1] = yi.astype(BF)

    v_stores = copies(v_sem, *[(v.at[1 - t0, :, :, u], v_hbm.at[:, :, u]) for u in range(2)])
    for u in range(2):
        two_loads[u].wait()

        def step_two(n, _):
            t, d = jnp.where(n < 2, 1 - t0, t0), n & 1
            vr = first[d, :, t, 0].reshape(2 * half, lanes)
            vi = first[d, :, t, 1].reshape(2 * half, lanes)
            yr, yi = complex_dot(two[0, halves[u], :], two[1, halves[u], :], vr, vi)
            v[t, d, 0, u] = yr.astype(BF)
            v[t, d, 1, u] = yi.astype(BF)
            return 0

        lax.fori_loop(0, 4, step_two, 0)
        v_stores[u].start()

    for load in held_loads:
        load.wait()
    part_stores = copies(part_sem, *[(part.at[u], part_hbm.at[u]) for u in range(2)])
    for u in range(2):
        vr = jnp.concatenate([v[t0, d0, 0, u], v[t0, 1 - d0, 0, u]], axis=0)
        vi = jnp.concatenate([v[t0, d0, 1, u], v[t0, 1 - d0, 1, u]], axis=0)
        part[u, 0], part[u, 1] = complex_dot(held[0], held[1], vr, vi)
        part_stores[u].start()
    for store in v_stores + part_stores:
        store.wait()


def chained(place, x, one, two, held):
    half = one.shape[1] // 2
    lanes = x.shape[5]
    rows = held[0].shape[1]
    v_shape = (2, 2, 2, half, lanes)
    part_shape = (2, 2, rows, lanes)
    sems = lambda count: pltpu.SemaphoreType.DMA((count,))
    return pl.pallas_call(
        chain_kernel,
        in_specs=[pl.BlockSpec(memory_space=pltpu.SMEM)] + anywhere(5),
        out_specs=anywhere(2),
        out_shape=[jax.ShapeDtypeStruct(v_shape, BF), jax.ShapeDtypeStruct(part_shape, F32)],
        scratch_shapes=[
            pltpu.VMEM((2, 2) + x.shape[:2] + x.shape[4:], BF),
            pltpu.VMEM(one.shape, BF),
            pltpu.VMEM(two.shape, BF),
            pltpu.VMEM((2, rows, 2 * half), BF),
            pltpu.VMEM((2,) + v_shape, BF),
            pltpu.VMEM((2,) + v_shape, BF),
            pltpu.VMEM(part_shape, F32),
        ] + [sems(4), sems(2), sems(2), sems(2), sems(2), sems(2)],
        cost_estimate=pl.CostEstimate(flops=112 * half * half * 2 * lanes, transcendentals=0, bytes_accessed=72 * half**2),
        name="chain",
    )(place, x, one, two, *held)


def join_kernel(place_ref, *refs):
    weights_hbm, (v_hbm, part_hbm, out), (w, v, part, sem) = refs[:2], refs[2:5], refs[5:]
    lanes = v.shape[4]
    inner = w.shape[2] // 2
    d0 = place_ref[1]
    w_loads = copies(sem, *[(weights_hbm[n], w.at[:, :, pl.ds(n * inner, inner)]) for n in range(2)])
    v_loads = [pltpu.make_async_copy(v_hbm.at[:, :, u], v.at[:, :, u], sem.at[2 + u]) for u in range(2)]
    p_loads = [pltpu.make_async_copy(part_hbm.at[u], part.at[u], sem.at[4 + u]) for u in range(2)]
    for load in [v_loads[0]] + w_loads + [p_loads[0], v_loads[1], p_loads[1]]:
        load.start()
    for load in w_loads:
        load.wait()
    for u in range(2):
        v_loads[u].wait()
        vr = jnp.concatenate([v[d0, 0, u], v[1 - d0, 0, u]], axis=0)
        vi = jnp.concatenate([v[d0, 1, u], v[1 - d0, 1, u]], axis=0)
        p_loads[u].wait()
        yr, yi = complex_dot(w[0], w[1], vr, vi)
        for r, y in enumerate((yr, yi)):
            out[:, (2 * r + u) * lanes:(2 * r + u + 1) * lanes] = (part[u, r] + y).astype(BF)


def joined(place, weights, v, part):
    rows, inner = weights[0].shape[1:]
    lanes = v.shape[4]
    return pl.pallas_call(
        join_kernel,
        in_specs=[pl.BlockSpec(memory_space=pltpu.SMEM)] + anywhere(4),
        out_specs=pl.BlockSpec(memory_space=pltpu.VMEM),
        out_shape=jax.ShapeDtypeStruct((rows, 4 * lanes), BF),
        scratch_shapes=[
            pltpu.VMEM((2, rows, 2 * inner), BF),
            pltpu.VMEM(v.shape, BF),
            pltpu.VMEM(part.shape, F32),
            pltpu.SemaphoreType.DMA((6,)),
        ],
        cost_estimate=pl.CostEstimate(flops=32 * rows * inner * lanes, transcendentals=0, bytes_accessed=24 * rows * inner),
        name="join",
    )(place, *weights, v, part)


def pick_kernel(own_ref, pick_ref, branch_hbm, out_hbm, held, sem, out_sem):
    spot = pick_ref[own_ref[0]]
    loads = copies(sem, *[(branch_hbm.at[spot, r, 0], held.at[r]) for r in range(2)])
    stores = copies(out_sem, *[(held.at[r], out_hbm.at[r]) for r in range(2)])
    for load in loads:
        load.start()
    for load, store in zip(loads, stores):
        load.wait()
        store.start()
    for store in stores:
        store.wait()


def picked(own, slice_pick, branch):
    smem = pl.BlockSpec(memory_space=pltpu.SMEM)
    return pl.pallas_call(
        pick_kernel,
        in_specs=[smem, smem] + anywhere(1),
        out_specs=anywhere(1)[0],
        out_shape=jax.ShapeDtypeStruct(branch.shape[1:2] + branch.shape[3:], BF),
        scratch_shapes=[
            pltpu.VMEM(branch.shape[1:2] + branch.shape[3:], BF),
            pltpu.SemaphoreType.DMA((2,)),
            pltpu.SemaphoreType.DMA((2,)),
        ],
        cost_estimate=pl.CostEstimate(flops=0, transcendentals=0, bytes_accessed=2 * branch.size),
        name="pick",
    )(own.reshape(1).astype(jnp.int32), slice_pick, branch)


def per_device(stem, branch_one, branch_two, branch_three, leg_orders, slice_pick):
    groups = lax.axis_size("modes")
    own = lax.axis_index("modes")
    side = groups // 2
    quarter = groups // 4
    extent = stem.shape[2]
    lanes = stem.shape[4]
    leg_width = branch_one.shape[2]
    top = own // side
    core = own % 2
    middle = (own // quarter == 1) | (own // quarter == 2)

    beside = [(i, i ^ 1) for i in range(groups)]
    swap = [(a * quarter + i, b * quarter + i) for a, b in ((1, 2), (2, 1)) for i in range(quarter)]
    cycle = [(a * quarter + i, b * quarter + i) for a, b in ((0, 2), (2, 3), (3, 1), (1, 0)) for i in range(quarter)]

    chosen = picked(own, slice_pick, branch_three)
    out_width = chosen.shape[1]
    share = out_width // groups
    chosen, stem = lax.optimization_barrier((chosen, stem))

    def move(value, route):
        return lax.ppermute(value, "modes", route)

    swapped = move(chosen, swap)
    near = move(chosen, beside)

    pieces = stem.reshape(2, extent, 2, side, 2, lanes).transpose(3, 0, 2, 4, 1, 5)
    halves = [list(range(side)), list(range(side, groups))]
    arrived = lax.all_to_all(pieces, "modes", 0, 0, tiled=True, axis_index_groups=halves)
    if extent % 16:
        arrived = arrived.transpose(1, 2, 3, 0, 4, 5).reshape(1, 2, 2, 2, side * extent, lanes)

    start = (top * (leg_width // 2)).reshape(1).astype(jnp.int32)
    place = jnp.stack([top, core]).astype(jnp.int32)
    one = turned(0, start, leg_width // 2, leg_orders, branch_one)
    two = turned(1, jnp.zeros_like(start), leg_width, leg_orders, branch_two)
    swapped, one, two = lax.optimization_barrier((swapped, one, two))
    other = move(jnp.where(middle, swapped, chosen), cycle)
    v, part = chained(place, arrived, one, two, (chosen, near))
    other, v = lax.optimization_barrier((other, v))
    far = move(other, beside)
    partial = joined(place, (other, far), v, part)
    spread = lax.all_to_all(partial.reshape(groups, share, 4 * lanes), "modes", 0, 0, tiled=True)
    total = jnp.sum(spread.reshape(side, 2, share, 4 * lanes).astype(F32), axis=0).astype(BF)
    return total.reshape(2, share, 2, 2, lanes).transpose(1, 2, 3, 0, 4)


def solution(mesh):
    in_specs = (
        P(None, "modes", None, None, "parts"),
        P(),
        P(),
        P(None, None, "modes", None, None),
        P(),
        P("parts"),
    )
    out_specs = P(("parts", "modes"), None, None, None, None)

    return jax.shard_map(per_device, mesh=mesh, in_specs=in_specs, out_specs=out_specs, check_vma=False)
```

time: 141 us -> 108 us (0.77)
  waiting for transfers between devices: 45.6 us -> 2.51 us
  starting transfers between devices: 9.4 us -> 22.8 us
  between operations: 1.99 us -> 0.09 us
  local copies, waits for them, and re-layouts: 7.7 us -> 5.83 us
    ppermute x3 -> x4, waiting for transfers between devices: 45.6 us -> 2.51 us  [move(): return lax.ppermute(value, 'modes', route)]
    ppermute x3 -> x4, starting transfers between devices: 4 us -> 17.4 us  [move(): return lax.ppermute(value, 'modes', route)]
    reshape x1, local copies, waits for them, and re-layouts: 1.83 us -> 0.08 us  [per_device(): return total.reshape(2, share, 2, 2, lanes).transpose(1, 2, 3, 0, 4)]
    pallas_call x3 -> x5, Pallas kernels: 42.8 us -> 43.9 us  [the longest x1 20.9 us: chained(): pl.pallas_call(chain_kernel, in_specs=[pl.BlockSpec(memory_space=pltpu.SM...]
    unnamed x7 -> x8, local copies, waits for them, and re-layouts: 2.93 us -> 2.32 us
  transfers between devices with their start and end apart: 4 -> 5, of which waited for: 1 -> 1; matrix products, arithmetic and copies ran while one was open for 1% -> 2% of each run, Pallas kernels for 24% -> 32%
where the time goes in v1:
time: 108 us
  Pallas kernels  43.9 us (41%)
  blocking collectives  31 us (29%)
  starting transfers between devices  22.8 us (21%)
  local copies, waits for them, and re-layouts  5.83 us (5%)
  waiting for transfers between devices  2.51 us (2%)
  other arithmetic  1.83 us (2%)
    all_to_all x1, blocking collectives, per_device(): lax.all_to_all(partial.reshape(groups, share, 4 * lanes), 'modes', 0, 0,...  31 us
    pallas_call x1, Pallas kernels, chained(): pl.pallas_call(chain_kernel, in_specs=[pl.BlockSpec(memory_space=pltpu.SM...  20.9 us
    ppermute x4, starting transfers between devices, move(): return lax.ppermute(value, 'modes', route)  17.4 us
    pallas_call x2, Pallas kernels, turned(): pl.pallas_call(lambda *refs: turn_kernel(row, *refs), in_specs=[smem, sme...  13.7 us
    pallas_call x1, Pallas kernels, joined(): pl.pallas_call(join_kernel, in_specs=[pl.BlockSpec(memory_space=pltpu.SME...  6.48 us
    all_to_all x1, starting transfers between devices, per_device(): lax.all_to_all(pieces, 'modes', 0, 0, tiled=True, axis_index_groups=halves)  5.4 us
    pallas_call x1, Pallas kernels, picked(): pl.pallas_call(pick_kernel, in_specs=[smem, smem] + anywhere(1), out_spec...  2.9 us
    ppermute x4, waiting for transfers between devices, move(): return lax.ppermute(value, 'modes', route)  2.51 us
  transfers between devices with their start and end apart: 5, of which 1 were waited for; matrix products, arithmetic and copies ran while one was open for 2% of the time, Pallas kernels for 32%

profile of v1, /device:TPU:1, one launch (start us, length us, event | category | flops | bytes accessed | tf_op | source)
XLA Modules:
  0.0 108.0 jit_solution(12393596603390880563)
XLA Ops:
  0.0 2.9 %pick.1.refs_0_ = bf16[2,512,512]{2,1,0:T(8,128)(2,1)} custom-call(s32[1]{0:T(128)} %bitcast.2.own_ref, s32[16]{0:T(128)} %pick_ref.1, bf16[2,2,1,512,512]{4,3,2,1,0:T(8,128)(2,1)} %branch_hbm.1), custom_call_target="tpu_custom_call" | custom-call | bytes 2097152 | tf_op jit(solution)/shard_map/pick/pallas_call | solution.py:217
  2.9 1.2 %copy.7 = bf16[2,1,64,32,256]{4,2,3,0,1:T(8,128)(2,1)S(1)} copy(bf16[2,1,64,32,256]{4,3,2,1,0:T(8,128)(2,1)S(1)} %copy-done.1) | data formatting | bytes 4194304 | tf_op jit(solution)/shard_map/optimization_barrier | solution.py:251
  4.1 1.5 %copy.11 = bf16[2,64,2,8,2,256]{5,1,4,2,0,3:T(8,128)(2,1)} copy(bf16[2,64,2,8,2,256]{5,1,4,3,2,0:T(8,128)(2,1)S(1)} %bitcast.11) | data formatting | bytes 4194304 | tf_op jit(solution)/shard_map/reshape | solution.py:259
  5.6 5.4 %all-to-all-start = ((bf16[8,2,2,2,64,256]{5,4,3,2,1,0:T(8,128)(2,1)}), bf16[8,2,2,2,64,256]{5,4,3,2,1,0:T(8,128)(2,1)S(1)}, u32[]{:S(2)}, u32[]{:S(2)}) async-start(bf16[8,2,2,2,64,256]{5,4,3,2,1,0:T(8,128)(2,1)} %bitcast.10), calls=%async_computation | async-start | bytes 4194304 | tf_op jit(solution)/shard_map/all_to_all | solution.py:261
  11.0 1.6 %collective-permute-start = (bf16[2,512,512]{2,1,0:T(8,128)(2,1)S(1)}, bf16[2,512,512]{2,1,0:T(8,128)(2,1)}, u32[]{:S(2)}, u32[]{:S(2)}) collective-permute-start(bf16[2,512,512]{2,1,0:T(8,128)(2,1)S(1)} %copy-done), channel_id=1, source_target_pairs={{4,8},{5,9},{6,10},{7,11},{8,4},{9,5},{10,6},{11,7},{20,24},{21,25... | collective-permute-start | bytes 3145736 | tf_op jit(solution)/shard_map/ppermute | solution.py:254
  12.6 0.0 collective-permute-start.2
  12.6 0.6 pad_add_fusion.place_ref
  13.2 5.7 %turn.2.one_hbm = bf16[2,1024,512]{2,1,0:T(8,128)(2,1)} custom-call(s32[1]{0:T(128)} %bitcast.3.refs_0_, s32[2,10]{1,0:T(2,128)} %refs_1_.3, bf16[2,1024,1024]{2,1,0:T(8,128)(2,1)} %refs_2_.2), custom_call_target="tpu_custom_call" | custom-call | flops 2147483648 | bytes 4194304 | tf_op jit(solution)/shard_map/turn/pallas_call | solution.py:61
  18.9 8.0 %turn.3.two_hbm = bf16[2,1024,1024]{2,1,0:T(8,128)(2,1)} custom-call(s32[1]{0:T(128)} %constant.48.clone.1.refs_0_, s32[2,10]{1,0:T(2,128)} %refs_1_.3, bf16[2,1024,1024]{2,1,0:T(8,128)(2,1)} %refs_2_.3), custom_call_target="tpu_custom_call" | custom-call | flops 4294967296 | bytes 4194304 | tf_op jit(solution)/shard_map/turn/pallas_call | solution.py:61
  26.9 0.0 collective-permute-done
  26.9 1.1 %broadcast_select_fusion = bf16[2,512,512]{2,1,0:T(8,128)(2,1)} fusion(bf16[2,512,512]{2,1,0:T(8,128)(2,1)} %collective-permute-done, bf16[2,512,512]{2,1,0:T(8,128)(2,1)S(1)} %copy-done, pred[]{:T(512)S(6)} %or.3), kind=kLoop, calls=%fused_computation.1 | loop fusion | flops 524288 | bytes 3145729 | tf_op jit(solution)/shard_map/jit(_where)/select_n | solution.py:270
  28.0 14.3 %collective-permute-start.1 = (bf16[2,512,512]{2,1,0:T(8,128)(2,1)}, bf16[2,512,512]{2,1,0:T(8,128)(2,1)}, u32[]{:S(2)}, u32[]{:S(2)}) collective-permute-start(bf16[2,512,512]{2,1,0:T(8,128)(2,1)} %broadcast_select_fusion), channel_id=1, source_target_pairs={{0,8},{1,9},{2,10},{3,11},{8,12},{9,13},{10,14},{11,15},{12,4},{13... | collective-permute-start | bytes 3145736 | tf_op jit(solution)/shard_map/ppermute | solution.py:254
  42.3 0.0 all-to-all-done.x_hbm
  42.3 1.3 %copy-done.2 = bf16[8,2,2,2,64,256]{5,4,3,2,1,0:T(8,128)(2,1)} copy-done((bf16[8,2,2,2,64,256]{5,4,3,2,1,0:T(8,128)(2,1)}, bf16[8,2,2,2,64,256]{5,4,3,2,1,0:T(8,128)(2,1)S(1)}, u32[]{:S(2)}) %copy-start.2) | copy-done | bytes 2097176
  43.6 20.9 %chain.1 = (bf16[2,2,2,512,256]{4,3,2,1,0:T(8,128)(2,1)}, f32[2,2,512,256]{3,2,1,0:T(8,128)}) custom-call(s32[2]{0:T(128)} %pad_add_fusion.place_ref, bf16[8,2,2,2,64,256]{5,4,3,2,1,0:T(8,128)(2,1)} %copy-done.2, bf16[2,1024,512]{2,1,0:T(8,128)(2,1)} %turn.2.one_hbm, bf16[2,1024,1024]{2,1,0:T(8,128)(2,1)} %turn.3.two_hbm, bf16[2,512,512]{2,1,0:T(8,128)(2,1)} %pick.1.refs_0_, ...), custom_call_target="tpu_custom_call" | custom-call | flops 15032385536 | bytes 18874368 | tf_op jit(solution)/shard_map/chain/pallas_call | solution.py:142
  64.5 0.0 collective-permute-done.1.refs_0_
  64.5 1.5 %collective-permute-start.3 = (bf16[2,512,512]{2,1,0:T(8,128)(2,1)}, bf16[2,512,512]{2,1,0:T(8,128)(2,1)S(1)}, u32[]{:S(2)}, u32[]{:S(2)}) collective-permute-start(bf16[2,512,512]{2,1,0:T(8,128)(2,1)} %collective-permute-done.1.refs_0_), channel_id=1, source_target_pairs={{0,1},{1,0},{2,3},{3,2},{4,5},{5,4},{6,7},{7,6},{8,9},{9,8},{10,11... | collective-permute-start | bytes 3145736 | tf_op jit(solution)/shard_map/ppermute | solution.py:254
  66.0 2.5 %collective-permute-done.3.refs_1_ = bf16[2,512,512]{2,1,0:T(8,128)(2,1)S(1)} collective-permute-done((bf16[2,512,512]{2,1,0:T(8,128)(2,1)}, bf16[2,512,512]{2,1,0:T(8,128)(2,1)S(1)}, u32[]{:S(2)}, u32[]{:S(2)}) %collective-permute-start.3) | collective-permute-done | bytes 1048608 | tf_op jit(solution)/shard_map/ppermute | solution.py:254
  68.5 1.0 copy-done.3
  69.5 6.5 %join.1 = bf16[512,1024]{1,0:T(8,128)(2,1)} custom-call(s32[2]{0:T(128)} %pad_add_fusion.place_ref, bf16[2,512,512]{2,1,0:T(8,128)(2,1)} %collective-permute-done.1.refs_0_, bf16[2,512,512]{2,1,0:T(8,128)(2,1)} %copy-done.3, bf16[2,2,2,512,256]{4,3,2,1,0:T(8,128)(2,1)} %get-tuple-element.21.refs_2_, f32[2,2,512,256]{3,2,1,0:T(8,128)} %get-tuple-element.22.refs_3_), custom_call_target="tpu_custom_call" | custom-call | flops 2147483648 | bytes 6291456 | tf_op jit(solution)/shard_map/join/pallas_call | solution.py:186
  76.0 31.0 %all_to_all.10 = bf16[16,32,1024]{2,1,0:T(8,128)(2,1)S(1)} all-to-all(bf16[16,32,1024]{2,1,0:T(8,128)(2,1)} %bitcast.13), channel_id=1, replica_groups=mesh['parts'=2,'modes'=16] {'modes'}, dimensions={0} | all-to-all | bytes 2097152 | tf_op jit(solution)/shard_map/all_to_all | solution.py:275
  106.9 0.2 reduce_sum.12
  107.1 0.1 reshape.23
  107.2 0.8 copy.9
  (7 shorter events, 0.0 us)
Async XLA Ops:
  0.0 2.9 %copy-start.1 = (bf16[2,1,64,32,256]{4,3,2,1,0:T(8,128)(2,1)S(1)}, bf16[2,1,64,32,256]{4,3,2,1,0:T(8,128)(2,1)}, u32[]{:S(2)}) copy-start(bf16[2,1,64,32,256]{4,3,2,1,0:T(8,128)(2,1)} %param.6) | copy-start | bytes 6291460
  5.6 5.4 %copy-start = (bf16[2,512,512]{2,1,0:T(8,128)(2,1)S(1)}, bf16[2,512,512]{2,1,0:T(8,128)(2,1)}, u32[]{:S(2)}) copy-start(bf16[2,512,512]{2,1,0:T(8,128)(2,1)} %pick.1.refs_0_) | copy-start | bytes 3145732
  5.6 36.7 %all-to-all-start = ((bf16[8,2,2,2,64,256]{5,4,3,2,1,0:T(8,128)(2,1)}), bf16[8,2,2,2,64,256]{5,4,3,2,1,0:T(8,128)(2,1)S(1)}, u32[]{:S(2)}, u32[]{:S(2)}) async-start(bf16[8,2,2,2,64,256]{5,4,3,2,1,0:T(8,128)(2,1)} %bitcast.10), calls=%async_computation | async-start | bytes 4194304 | tf_op jit(solution)/shard_map/all_to_all | solution.py:261
  11.0 15.9 %collective-permute-start = (bf16[2,512,512]{2,1,0:T(8,128)(2,1)S(1)}, bf16[2,512,512]{2,1,0:T(8,128)(2,1)}, u32[]{:S(2)}, u32[]{:S(2)}) collective-permute-start(bf16[2,512,512]{2,1,0:T(8,128)(2,1)S(1)} %copy-done), channel_id=1, source_target_pairs={{4,8},{5,9},{6,10},{7,11},{8,4},{9,5},{10,6},{11,7},{20,24},{21,25... | collective-permute-start | bytes 3145736 | tf_op jit(solution)/shard_map/ppermute | solution.py:254
  12.6 29.7 %collective-permute-start.2 = (bf16[2,512,512]{2,1,0:T(8,128)(2,1)S(1)}, bf16[2,512,512]{2,1,0:T(8,128)(2,1)}, u32[]{:S(2)}, u32[]{:S(2)}) collective-permute-start(bf16[2,512,512]{2,1,0:T(8,128)(2,1)S(1)} %copy-done), channel_id=1, source_target_pairs={{0,1},{1,0},{2,3},{3,2},{4,5},{5,4},{6,7},{7,6},{8,9},{9,8},{10,11... | collective-permute-start | bytes 3145736 | tf_op jit(solution)/shard_map/ppermute | solution.py:254
  28.0 36.5 %collective-permute-start.1 = (bf16[2,512,512]{2,1,0:T(8,128)(2,1)}, bf16[2,512,512]{2,1,0:T(8,128)(2,1)}, u32[]{:S(2)}, u32[]{:S(2)}) collective-permute-start(bf16[2,512,512]{2,1,0:T(8,128)(2,1)} %broadcast_select_fusion), channel_id=1, source_target_pairs={{0,8},{1,9},{2,10},{3,11},{8,12},{9,13},{10,14},{11,15},{12,4},{13... | collective-permute-start | bytes 3145736 | tf_op jit(solution)/shard_map/ppermute | solution.py:254
  42.3 1.3 %copy-start.2 = (bf16[8,2,2,2,64,256]{5,4,3,2,1,0:T(8,128)(2,1)}, bf16[8,2,2,2,64,256]{5,4,3,2,1,0:T(8,128)(2,1)S(1)}, u32[]{:S(2)}) copy-start(bf16[8,2,2,2,64,256]{5,4,3,2,1,0:T(8,128)(2,1)S(1)} %all-to-all-done.x_hbm) | copy-start | bytes 6291460
  64.5 4.0 %collective-permute-start.3 = (bf16[2,512,512]{2,1,0:T(8,128)(2,1)}, bf16[2,512,512]{2,1,0:T(8,128)(2,1)S(1)}, u32[]{:S(2)}, u32[]{:S(2)}) collective-permute-start(bf16[2,512,512]{2,1,0:T(8,128)(2,1)} %collective-permute-done.1.refs_0_), channel_id=1, source_target_pairs={{0,1},{1,0},{2,3},{3,2},{4,5},{5,4},{6,7},{7,6},{8,9},{9,8},{10,11... | collective-permute-start | bytes 3145736 | tf_op jit(solution)/shard_map/ppermute | solution.py:254
  68.5 1.0 copy-start.3

commit v2 on v1

--- a/solution.py
+++ b/solution.py
@@ -16,6 +16,14 @@
 
 def copies(sem, *pairs):
     return [pltpu.make_async_copy(src, dst, sem.at[n]) for n, (src, dst) in enumerate(pairs)]
+
+
+def params(mib):
+    return pltpu.CompilerParams(vmem_limit_bytes=mib << 20)
+
+
+def inside(count):
+    return [pl.BlockSpec(memory_space=pltpu.VMEM) for _ in range(count)]
 
 
 def anywhere(count):
@@ -71,65 +79,56 @@
             pltpu.SemaphoreType.DMA((4,)),
         ],
         cost_estimate=pl.CostEstimate(flops=4 * width * leg_width**2, transcendentals=0, bytes_accessed=4 * leg_width**2),
+        compiler_params=params(16),
         name="turn",
     )(start, orders, branch)
 
 
-def chain_kernel(place_ref, x_hbm, one_hbm, two_hbm, *refs):
-    held_hbm, (v_hbm, part_hbm) = refs[:2], refs[2:4]
-    x, one, two, held, first, v, part, x_sem, one_sem, two_sem, held_sem, v_sem, part_sem = refs[4:]
+def chain_kernel(place_ref, x, one_hbm, two_hbm, *refs):
+    held_hbm, (v_out, part) = refs[:2], refs[2:4]
+    one, two, held, first, v, one_sem, two_sem, held_sem = refs[4:]
     half = one.shape[1] // 2
     lanes = x.shape[5]
-    inner = x.shape[2] * x.shape[4]
+    inner = x.shape[0] * x.shape[4]
     halves = [pl.ds(u * half, half) for u in range(2)]
     t0, d0 = place_ref[0], place_ref[1]
     spots = [(d, a) for d in range(2) for a in range(2)]
-    x_loads = copies(x_sem, *[(x_hbm.at[:, :, a, d], x.at[d, a]) for d, a in spots])
     one_loads = copies(one_sem, *[(one_hbm.at[:, rows], one.at[:, rows]) for rows in halves])
     two_loads = copies(two_sem, *[(two_hbm.at[:, rows], two.at[:, rows]) for rows in halves])
     held_loads = copies(held_sem, *[(held_hbm[n], held.at[:, :, pl.ds(n * half, half)]) for n in range(2)])
-    x_loads[0].start()
     one_loads[0].start()
-    for load in x_loads[1:] + one_loads[1:] + two_loads + held_loads:
+    for load in one_loads[1:] + two_loads + held_loads:
         load.start()
 
     for t in range(2):
         one_loads[t].wait()
         for d, a in spots:
-            if t == 0:
-                x_loads[2 * d + a].wait()
-            vr = x[d, a, :, 0].reshape(inner, lanes)
-            vi = x[d, a, :, 1].reshape(inner, lanes)
+            vr = x[:, 0, a, d].reshape(inner, lanes)
+            vi = x[:, 1, a, d].reshape(inner, lanes)
             yr, yi = complex_dot(one[0, halves[t], :], one[1, halves[t], :], vr, vi)
             first[d, a, t, 0] = yr.astype(BF)
             first[d, a, t, 1] = yi.astype(BF)
 
-    v_stores = copies(v_sem, *[(v.at[1 - t0, :, :, u], v_hbm.at[:, :, u]) for u in range(2)])
     for u in range(2):
         two_loads[u].wait()
 
         def step_two(n, _):
-            t, d = jnp.where(n < 2, 1 - t0, t0), n & 1
-            vr = first[d, :, t, 0].reshape(2 * half, lanes)
-            vi = first[d, :, t, 1].reshape(2 * half, lanes)
-            yr, yi = complex_dot(two[0, halves[u], :], two[1, halves[u], :], vr, vi)
-            v[t, d, 0, u] = yr.astype(BF)
-            v[t, d, 1, u] = yi.astype(BF)
+            for t, out in ((t0, v), (1 - t0, v_out)):
+                vr = first[n, :, t, 0].reshape(2 * half, lanes)
+                vi = first[n, :, t, 1].reshape(2 * half, lanes)
+                yr, yi = complex_dot(two[0, halves[u], :], two[1, halves[u], :], vr, vi)
+                out[n, 0, u] = yr.astype(BF)
+                out[n, 1, u] = yi.astype(BF)
             return 0
 
-        lax.fori_loop(0, 4, step_two, 0)
-        v_stores[u].start()
+        lax.fori_loop(0, 2, step_two, 0)
 
     for load in held_loads:
         load.wait()
-    part_stores = copies(part_sem, *[(part.at[u], part_hbm.at[u]) for u in range(2)])
     for u in range(2):
-        vr = jnp.concatenate([v[t0, d0, 0, u], v[t0, 1 - d0, 0, u]], axis=0)
-        vi = jnp.concatenate([v[t0, d0, 1, u], v[t0, 1 - d0, 1, u]], axis=0)
+        vr = jnp.concatenate([v[d0, 0, u], v[1 - d0, 0, u]], axis=0)
+        vi = jnp.concatenate([v[d0, 1, u], v[1 - d0, 1, u]], axis=0)
         part[u, 0], part[u, 1] = complex_dot(held[0], held[1], vr, vi)
-        part_stores[u].start()
-    for store in v_stores + part_stores:
-        store.wait()
 
 
 def chained(place, x, one, two, held):
@@ -141,41 +140,30 @@
     sems = lambda count: pltpu.SemaphoreType.DMA((count,))
     return pl.pallas_call(
         chain_kernel,
-        in_specs=[pl.BlockSpec(memory_space=pltpu.SMEM)] + anywhere(5),
-        out_specs=anywhere(2),
-        out_shape=[jax.ShapeDtypeStruct(v_shape, BF), jax.ShapeDtypeStruct(part_shape, F32)],
+        in_specs=[pl.BlockSpec(memory_space=pltpu.SMEM)] + inside(1) + anywhere(4),
+        out_specs=inside(2),
+        out_shape=[pltpu.VMEM(v_shape, BF), pltpu.VMEM(part_shape, F32)],
         scratch_shapes=[
-            pltpu.VMEM((2, 2) + x.shape[:2] + x.shape[4:], BF),
             pltpu.VMEM(one.shape, BF),
             pltpu.VMEM(two.shape, BF),
             pltpu.VMEM((2, rows, 2 * half), BF),
             pltpu.VMEM((2,) + v_shape, BF),
-            pltpu.VMEM((2,) + v_shape, BF),
-            pltpu.VMEM(part_shape, F32),
-        ] + [sems(4), sems(2), sems(2), sems(2), sems(2), sems(2)],
+            pltpu.VMEM(v_shape, BF),
+        ] + [sems(2), sems(2), sems(2)],
         cost_estimate=pl.CostEstimate(flops=112 * half * half * 2 * lanes, transcendentals=0, bytes_accessed=72 * half**2),
+        compiler_params=params(28),
         name="chain",
     )(place, x, one, two, *held)
 
 
-def join_kernel(place_ref, *refs):
-    weights_hbm, (v_hbm, part_hbm, out), (w, v, part, sem) = refs[:2], refs[2:5], refs[5:]
+def join_kernel(place_ref, w_own, w_other, v, part, out):
     lanes = v.shape[4]
-    inner = w.shape[2] // 2
     d0 = place_ref[1]
-    w_loads = copies(sem, *[(weights_hbm[n], w.at[:, :, pl.ds(n * inner, inner)]) for n in range(2)])
-    v_loads = [pltpu.make_async_copy(v_hbm.at[:, :, u], v.at[:, :, u], sem.at[2 + u]) for u in range(2)]
-    p_loads = [pltpu.make_async_copy(part_hbm.at[u], part.at[u], sem.at[4 + u]) for u in range(2)]
-    for load in [v_loads[0]] + w_loads + [p_loads[0], v_loads[1], p_loads[1]]:
-        load.start()
-    for load in w_loads:
-        load.wait()
+    wr, wi = (jnp.concatenate([w_own[r], w_other[r]], axis=1) for r in range(2))
     for u in range(2):
-        v_loads[u].wait()
         vr = jnp.concatenate([v[d0, 0, u], v[1 - d0, 0, u]], axis=0)
         vi = jnp.concatenate([v[d0, 1, u], v[1 - d0, 1, u]], axis=0)
-        p_loads[u].wait()
-        yr, yi = complex_dot(w[0], w[1], vr, vi)
+        yr, yi = complex_dot(wr, wi, vr, vi)
         for r, y in enumerate((yr, yi)):
             out[:, (2 * r + u) * lanes:(2 * r + u + 1) * lanes] = (part[u, r] + y).astype(BF)
 
@@ -185,16 +173,11 @@
     lanes = v.shape[4]
     return pl.pallas_call(
         join_kernel,
-        in_specs=[pl.BlockSpec(memory_space=pltpu.SMEM)] + anywhere(4),
-        out_specs=pl.BlockSpec(memory_space=pltpu.VMEM),
+        in_specs=[pl.BlockSpec(memory_space=pltpu.SMEM)] + inside(4),
+        out_specs=inside(1)[0],
         out_shape=jax.ShapeDtypeStruct((rows, 4 * lanes), BF),
-        scratch_shapes=[
-            pltpu.VMEM((2, rows, 2 * inner), BF),
-            pltpu.VMEM(v.shape, BF),
-            pltpu.VMEM(part.shape, F32),
-            pltpu.SemaphoreType.DMA((6,)),
-        ],
         cost_estimate=pl.CostEstimate(flops=32 * rows * inner * lanes, transcendentals=0, bytes_accessed=24 * rows * inner),
+        compiler_params=params(16),
         name="join",
     )(place, *weights, v, part)
 
@@ -225,6 +208,7 @@
             pltpu.SemaphoreType.DMA((2,)),
         ],
         cost_estimate=pl.CostEstimate(flops=0, transcendentals=0, bytes_accessed=2 * branch.size),
+        compiler_params=params(4),
         name="pick",
     )(own.reshape(1).astype(jnp.int32), slice_pick, branch)
 

time: 108 us -> 105 us (0.972)
  Pallas kernels: 43.9 us -> 33 us
  local copies, waits for them, and re-layouts: 5.83 us -> 16 us
  starting transfers between devices: 22.8 us -> 20.7 us
    unnamed x8 -> x20, local copies, waits for them, and re-layouts: 2.32 us -> 12.3 us
    pallas_call x1, Pallas kernels: 20.9 us -> 17.6 us  [chained(): pl.pallas_call(chain_kernel, in_specs=[pl.BlockSpec(memory_space=pltpu.SM...]
    pallas_call x1, Pallas kernels: 6.48 us -> 3.65 us  [joined(): pl.pallas_call(join_kernel, in_specs=[pl.BlockSpec(memory_space=pltpu.SME...]
    pallas_call x2, Pallas kernels: 13.7 us -> 11 us  [turned(): pl.pallas_call(lambda *refs: turn_kernel(row, *refs), in_specs=[smem, sme...]
    pallas_call x1, Pallas kernels: 2.9 us -> 0.73 us  [picked(): pl.pallas_call(pick_kernel, in_specs=[smem, smem] + anywhere(1), out_spec...]
    ppermute x4, starting transfers between devices: 17.4 us -> 15.3 us  [move(): return lax.ppermute(value, 'modes', route)]
  transfers between devices with their start and end apart: 5 -> 5, of which waited for: 1 -> 2; matrix products, arithmetic and copies ran while one was open for 2% -> 1% of each run, Pallas kernels for 32% -> 27%
where the time goes in v2:
time: 105 us
  Pallas kernels  33 us (31%)
  blocking collectives  30.8 us (29%)
  starting transfers between devices  20.7 us (20%)
  local copies, waits for them, and re-layouts  16 us (15%)
  waiting for transfers between devices  3.09 us (3%)
  other arithmetic  1.35 us (1%)
    all_to_all x1, blocking collectives, per_device(): lax.all_to_all(partial.reshape(groups, share, 4 * lanes), 'modes', 0, 0,...  30.8 us
    pallas_call x1, Pallas kernels, chained(): pl.pallas_call(chain_kernel, in_specs=[pl.BlockSpec(memory_space=pltpu.SM...  17.6 us
    ppermute x4, starting transfers between devices, move(): return lax.ppermute(value, 'modes', route)  15.3 us
    unnamed x20, local copies, waits for them, and re-layouts  12.3 us
    pallas_call x2, Pallas kernels, turned(): pl.pallas_call(lambda *refs: turn_kernel(row, *refs), in_specs=[smem, sme...  11 us
    all_to_all x1, starting transfers between devices, per_device(): lax.all_to_all(pieces, 'modes', 0, 0, tiled=True, axis_index_groups=halves)  5.4 us
    pallas_call x1, Pallas kernels, joined(): pl.pallas_call(join_kernel, in_specs=[pl.BlockSpec(memory_space=pltpu.SME...  3.65 us
    ppermute x4, waiting for transfers between devices, move(): return lax.ppermute(value, 'modes', route)  3.09 us
  transfers between devices with their start and end apart: 5, of which 2 were waited for; matrix products, arithmetic and copies ran while one was open for 1% of the time, Pallas kernels for 27%

profile of v2, /device:TPU:1, one launch (start us, length us, event | category | flops | bytes accessed | tf_op | source)
XLA Modules:
  0.0 105.0 jit_solution(11099806170331758177)
XLA Ops:
  0.0 1.6 %copy-done = bf16[2,2,1,512,512]{4,3,2,1,0:T(8,128)(2,1)S(1)} copy-done((bf16[2,2,1,512,512]{4,3,2,1,0:T(8,128)(2,1)S(1)}, bf16[2,2,1,512,512]{4,3,2,1,0:T(8,128)(2,1)}, u32[]{:S(2)}) %copy-start) | copy-done | bytes 2097176
  1.6 0.7 copy-done.1
  2.2 0.7 pick.1.refs_0_
  3.0 0.9 copy-done.9
  3.8 1.2 %copy.7 = bf16[2,1,64,32,256]{4,2,3,0,1:T(8,128)(2,1)S(1)} copy(bf16[2,1,64,32,256]{4,3,2,1,0:T(8,128)(2,1)S(1)} %copy-done.9) | data formatting | bytes 4194304 | tf_op jit(solution)/shard_map/optimization_barrier | solution.py:235
  5.0 1.6 %copy.11 = bf16[2,64,2,8,2,256]{5,1,4,2,0,3:T(8,128)(2,1)} copy(bf16[2,64,2,8,2,256]{5,1,4,3,2,0:T(8,128)(2,1)S(1)} %bitcast.13) | data formatting | bytes 4194304 | tf_op jit(solution)/shard_map/reshape | solution.py:243
  6.6 5.4 %all-to-all-start = ((bf16[8,2,2,2,64,256]{5,4,3,2,1,0:T(8,128)(2,1)}), bf16[8,2,2,2,64,256]{5,4,3,2,1,0:T(8,128)(2,1)S(1)}, u32[]{:S(2)}, u32[]{:S(2)}) async-start(bf16[8,2,2,2,64,256]{5,4,3,2,1,0:T(8,128)(2,1)} %bitcast.12), calls=%async_computation | async-start | bytes 4194304 | tf_op jit(solution)/shard_map/all_to_all | solution.py:245
  12.0 1.6 %collective-permute-start = (bf16[2,512,512]{2,1,0:T(8,128)(2,1)S(1)}, bf16[2,512,512]{2,1,0:T(8,128)(2,1)}, u32[]{:S(2)}, u32[]{:S(2)}) collective-permute-start(bf16[2,512,512]{2,1,0:T(8,128)(2,1)S(1)} %pick.1.refs_0_), channel_id=1, source_target_pairs={{4,8},{5,9},{6,10},{7,11},{8,4},{9,5},{10,6},{11,7},{20,24},{21,25... | collective-permute-start | bytes 3145736 | tf_op jit(solution)/shard_map/ppermute | solution.py:238
  13.7 2.2 %copy-done.2 = bf16[2,1024,1024]{2,1,0:T(8,128)(2,1)S(1)} copy-done((bf16[2,1024,1024]{2,1,0:T(8,128)(2,1)S(1)}, bf16[2,1024,1024]{2,1,0:T(8,128)(2,1)}, u32[]{:S(2)}) %copy-start.2) | copy-done | bytes 4194328
  15.9 4.3 %turn.2.one_hbm = bf16[2,1024,512]{2,1,0:T(8,128)(2,1)S(1)} custom-call(s32[1]{0:T(128)} %bitcast.3.refs_0_, s32[2,10]{1,0:T(2,128)S(1)} %copy-done.4, bf16[2,1024,1024]{2,1,0:T(8,128)(2,1)S(1)} %copy-done.2), custom_call_target="tpu_custom_call" | custom-call | flops 2147483648 | bytes 4194304 | tf_op jit(solution)/shard_map/turn/pallas_call | solution.py:69
  20.2 1.3 %copy-done.5 = bf16[2,1024,512]{2,1,0:T(8,128)(2,1)} copy-done((bf16[2,1024,512]{2,1,0:T(8,128)(2,1)}, bf16[2,1024,512]{2,1,0:T(8,128)(2,1)S(1)}, u32[]{:S(2)}) %copy-start.5) | copy-done | bytes 2097176
  21.5 6.8 %turn.3.two_hbm = bf16[2,1024,1024]{2,1,0:T(8,128)(2,1)S(1)} custom-call(s32[1]{0:T(128)} %constant.48.clone.1.refs_0_, s32[2,10]{1,0:T(2,128)S(1)} %copy-done.4, bf16[2,1024,1024]{2,1,0:T(8,128)(2,1)S(1)} %copy-done.3), custom_call_target="tpu_custom_call" | custom-call | flops 4294967296 | bytes 4194304 | tf_op jit(solution)/shard_map/turn/pallas_call | solution.py:69
  28.3 1.9 %copy-done.7 = bf16[2,1024,1024]{2,1,0:T(8,128)(2,1)} copy-done((bf16[2,1024,1024]{2,1,0:T(8,128)(2,1)}, bf16[2,1024,1024]{2,1,0:T(8,128)(2,1)S(1)}, u32[]{:S(2)}) %copy-start.7) | copy-done | bytes 4194328
  30.3 1.1 %broadcast_select_fusion = bf16[2,512,512]{2,1,0:T(8,128)(2,1)} fusion(bf16[2,512,512]{2,1,0:T(8,128)(2,1)} %collective-permute-done, bf16[2,512,512]{2,1,0:T(8,128)(2,1)S(1)} %pick.1.refs_0_, pred[]{:T(512)S(6)} %or.3), kind=kLoop, calls=%fused_computation.1 | loop fusion | flops 524288 | bytes 3145729 | tf_op jit(solution)/shard_map/jit(_where)/select_n | solution.py:254
  31.4 12.0 %collective-permute-start.1 = (bf16[2,512,512]{2,1,0:T(8,128)(2,1)}, bf16[2,512,512]{2,1,0:T(8,128)(2,1)}, u32[]{:S(2)}, u32[]{:S(2)}) collective-permute-start(bf16[2,512,512]{2,1,0:T(8,128)(2,1)} %broadcast_select_fusion), channel_id=1, source_target_pairs={{0,8},{1,9},{2,10},{3,11},{8,12},{9,13},{10,14},{11,15},{12,4},{13... | collective-permute-start | bytes 3145736 | tf_op jit(solution)/shard_map/ppermute | solution.py:238
  43.4 1.6 %copy-done.6 = bf16[2,1024,512]{2,1,0:T(8,128)(2,1)S(1)} copy-done((bf16[2,1024,512]{2,1,0:T(8,128)(2,1)S(1)}, bf16[2,1024,512]{2,1,0:T(8,128)(2,1)}, u32[]{:S(2)}) %copy-start.6) | copy-done | bytes 2097176
  45.0 2.2 %copy-done.8 = bf16[2,1024,1024]{2,1,0:T(8,128)(2,1)S(1)} copy-done((bf16[2,1024,1024]{2,1,0:T(8,128)(2,1)S(1)}, bf16[2,1024,1024]{2,1,0:T(8,128)(2,1)}, u32[]{:S(2)}) %copy-start.8) | copy-done | bytes 4194328
  47.1 17.6 %chain.1 = (bf16[2,2,2,512,256]{4,3,2,1,0:T(8,128)(2,1)S(1)}, f32[2,2,512,256]{3,2,1,0:T(8,128)S(1)}) custom-call(s32[2]{0:T(128)S(1)} %pad_add_fusion.place_ref, bf16[8,2,2,2,64,256]{5,4,3,2,1,0:T(8,128)(2,1)S(1)} %all-to-all-done.x, bf16[2,1024,512]{2,1,0:T(8,128)(2,1)S(1)} %copy-done.6, bf16[2,1024,1024]{2,1,0:T(8,128)(2,1)S(1)} %copy-done.8, ...), custom_call_target="tpu_custom_call" | custom-call | flops 15032385536 | bytes 18874368 | tf_op jit(solution)/shard_map/chain/pallas_call | solution.py:141
  64.7 0.6 collective-permute-done.1.w_own
  65.3 1.7 %collective-permute-start.3 = (bf16[2,512,512]{2,1,0:T(8,128)(2,1)}, bf16[2,512,512]{2,1,0:T(8,128)(2,1)S(1)}, u32[]{:S(2)}, u32[]{:S(2)}) collective-permute-start(bf16[2,512,512]{2,1,0:T(8,128)(2,1)} %collective-permute-done.1.w_own), channel_id=1, source_target_pairs={{0,1},{1,0},{2,3},{3,2},{4,5},{5,4},{6,7},{7,6},{8,9},{9,8},{10,11... | collective-permute-start | bytes 3145736 | tf_op jit(solution)/shard_map/ppermute | solution.py:238
  67.0 2.5 %collective-permute-done.3.w_other = bf16[2,512,512]{2,1,0:T(8,128)(2,1)S(1)} collective-permute-done((bf16[2,512,512]{2,1,0:T(8,128)(2,1)}, bf16[2,512,512]{2,1,0:T(8,128)(2,1)S(1)}, u32[]{:S(2)}, u32[]{:S(2)}) %collective-permute-start.3) | collective-permute-done | bytes 1048608 | tf_op jit(solution)/shard_map/ppermute | solution.py:238
  69.5 3.6 %join.1 = bf16[512,1024]{1,0:T(8,128)(2,1)S(1)} custom-call(s32[2]{0:T(128)S(1)} %pad_add_fusion.place_ref, bf16[2,512,512]{2,1,0:T(8,128)(2,1)} %collective-permute-done.1.w_own, bf16[2,512,512]{2,1,0:T(8,128)(2,1)S(1)} %collective-permute-done.3.w_other, bf16[2,2,2,512,256]{4,3,2,1,0:T(8,128)(2,1)S(1)} %get-tuple-element.21.v, ...), custom_call_target="tpu_custom_call" | custom-call | flops 2147483648 | bytes 6291456 | tf_op jit(solution)/shard_map/join/pallas_call | solution.py:174
  73.2 30.8 %all_to_all.10 = bf16[16,32,1024]{2,1,0:T(8,128)(2,1)S(1)} all-to-all(bf16[16,32,1024]{2,1,0:T(8,128)(2,1)S(1)} %bitcast.11), channel_id=1, replica_groups=mesh['parts'=2,'modes'=16] {'modes'}, dimensions={0} | all-to-all | bytes 2097152 | tf_op jit(solution)/shard_map/all_to_all | solution.py:259
  104.2 0.8 copy.9
  (19 shorter events, 0.4 us)
Async XLA Ops:
  0.0 1.6 %copy-start = (bf16[2,2,1,512,512]{4,3,2,1,0:T(8,128)(2,1)S(1)}, bf16[2,2,1,512,512]{4,3,2,1,0:T(8,128)(2,1)}, u32[]{:S(2)}) copy-start(bf16[2,2,1,512,512]{4,3,2,1,0:T(8,128)(2,1)} %branch_hbm.1) | copy-start | bytes 6291460
  1.6 0.7 copy-start.1
  2.2 1.6 %copy-start.9 = (bf16[2,1,64,32,256]{4,3,2,1,0:T(8,128)(2,1)S(1)}, bf16[2,1,64,32,256]{4,3,2,1,0:T(8,128)(2,1)}, u32[]{:S(2)}) copy-start(bf16[2,1,64,32,256]{4,3,2,1,0:T(8,128)(2,1)} %param.6) | copy-start | bytes 6291460
  6.6 7.1 %copy-start.4 = (s32[2,10]{1,0:T(2,128)S(1)}, s32[2,10]{1,0:T(2,128)}, u32[]{:S(2)}) copy-start(s32[2,10]{1,0:T(2,128)} %refs_1_.3) | copy-start | bytes 244
  6.6 36.7 %all-to-all-start = ((bf16[8,2,2,2,64,256]{5,4,3,2,1,0:T(8,128)(2,1)}), bf16[8,2,2,2,64,256]{5,4,3,2,1,0:T(8,128)(2,1)S(1)}, u32[]{:S(2)}, u32[]{:S(2)}) async-start(bf16[8,2,2,2,64,256]{5,4,3,2,1,0:T(8,128)(2,1)} %bitcast.12), calls=%async_computation | async-start | bytes 4194304 | tf_op jit(solution)/shard_map/all_to_all | solution.py:245
  12.0 18.2 %collective-permute-start = (bf16[2,512,512]{2,1,0:T(8,128)(2,1)S(1)}, bf16[2,512,512]{2,1,0:T(8,128)(2,1)}, u32[]{:S(2)}, u32[]{:S(2)}) collective-permute-start(bf16[2,512,512]{2,1,0:T(8,128)(2,1)S(1)} %pick.1.refs_0_), channel_id=1, source_target_pairs={{4,8},{5,9},{6,10},{7,11},{8,4},{9,5},{10,6},{11,7},{20,24},{21,25... | collective-permute-start | bytes 3145736 | tf_op jit(solution)/shard_map/ppermute | solution.py:238
  13.6 29.7 %collective-permute-start.2 = (bf16[2,512,512]{2,1,0:T(8,128)(2,1)S(1)}, bf16[2,512,512]{2,1,0:T(8,128)(2,1)}, u32[]{:S(2)}, u32[]{:S(2)}) collective-permute-start(bf16[2,512,512]{2,1,0:T(8,128)(2,1)S(1)} %pick.1.refs_0_), channel_id=1, source_target_pairs={{0,1},{1,0},{2,3},{3,2},{4,5},{5,4},{6,7},{7,6},{8,9},{9,8},{10,11... | collective-permute-start | bytes 3145736 | tf_op jit(solution)/shard_map/ppermute | solution.py:238
  13.7 2.2 %copy-start.2 = (bf16[2,1024,1024]{2,1,0:T(8,128)(2,1)S(1)}, bf16[2,1024,1024]{2,1,0:T(8,128)(2,1)}, u32[]{:S(2)}) copy-start(bf16[2,1024,1024]{2,1,0:T(8,128)(2,1)} %refs_2_.2) | copy-start | bytes 12582916
  15.9 5.6 %copy-start.3 = (bf16[2,1024,1024]{2,1,0:T(8,128)(2,1)S(1)}, bf16[2,1024,1024]{2,1,0:T(8,128)(2,1)}, u32[]{:S(2)}) copy-start(bf16[2,1024,1024]{2,1,0:T(8,128)(2,1)} %refs_2_.3) | copy-start | bytes 12582916
  20.2 1.3 %copy-start.5 = (bf16[2,1024,512]{2,1,0:T(8,128)(2,1)}, bf16[2,1024,512]{2,1,0:T(8,128)(2,1)S(1)}, u32[]{:S(2)}) copy-start(bf16[2,1024,512]{2,1,0:T(8,128)(2,1)S(1)} %turn.2.one_hbm) | copy-start | bytes 6291460
  28.3 1.9 %copy-start.7 = (bf16[2,1024,1024]{2,1,0:T(8,128)(2,1)}, bf16[2,1024,1024]{2,1,0:T(8,128)(2,1)S(1)}, u32[]{:S(2)}) copy-start(bf16[2,1024,1024]{2,1,0:T(8,128)(2,1)S(1)} %turn.3.two_hbm) | copy-start | bytes 12582916
  31.4 34.0 %collective-permute-start.1 = (bf16[2,512,512]{2,1,0:T(8,128)(2,1)}, bf16[2,512,512]{2,1,0:T(8,128)(2,1)}, u32[]{:S(2)}, u32[]{:S(2)}) collective-permute-start(bf16[2,512,512]{2,1,0:T(8,128)(2,1)} %broadcast_select_fusion), channel_id=1, source_target_pairs={{0,8},{1,9},{2,10},{3,11},{8,12},{9,13},{10,14},{11,15},{12,4},{13... | collective-permute-start | bytes 3145736 | tf_op jit(solution)/shard_map/ppermute | solution.py:238
  43.4 1.6 %copy-start.6 = (bf16[2,1024,512]{2,1,0:T(8,128)(2,1)S(1)}, bf16[2,1024,512]{2,1,0:T(8,128)(2,1)}, u32[]{:S(2)}) copy-start(bf16[2,1024,512]{2,1,0:T(8,128)(2,1)} %copy-done.5) | copy-start | bytes 6291460
  45.0 2.2 %copy-start.8 = (bf16[2,1024,1024]{2,1,0:T(8,128)(2,1)S(1)}, bf16[2,1024,1024]{2,1,0:T(8,128)(2,1)}, u32[]{:S(2)}) copy-start(bf16[2,1024,1024]{2,1,0:T(8,128)(2,1)} %copy-done.7) | copy-start | bytes 12582916
  65.3 4.2 %collective-permute-start.3 = (bf16[2,512,512]{2,1,0:T(8,128)(2,1)}, bf16[2,512,512]{2,1,0:T(8,128)(2,1)S(1)}, u32[]{:S(2)}, u32[]{:S(2)}) collective-permute-start(bf16[2,512,512]{2,1,0:T(8,128)(2,1)} %collective-permute-done.1.w_own), channel_id=1, source_target_pairs={{0,1},{1,0},{2,3},{3,2},{4,5},{5,4},{6,7},{7,6},{8,9},{9,8},{10,11... | collective-permute-start | bytes 3145736 | tf_op jit(solution)/shard_map/ppermute | solution.py:238

commit v3 on v2

--- a/solution.py
+++ b/solution.py
@@ -27,7 +27,7 @@
 
 
 def anywhere(count):
-    return [pl.BlockSpec(memory_space=pl.ANY) for _ in range(count)]
+    return [pl.BlockSpec(memory_space=pltpu.HBM) for _ in range(count)]
 
 
 def complex_dot(wr, wi, vr, vi):
@@ -153,33 +153,46 @@
         cost_estimate=pl.CostEstimate(flops=112 * half * half * 2 * lanes, transcendentals=0, bytes_accessed=72 * half**2),
         compiler_params=params(28),
         name="chain",
-    )(place, x, one, two, *held)
-
-
-def join_kernel(place_ref, w_own, w_other, v, part, out):
+    )(place, x, *[pltpu.with_memory_space_constraint(value, pltpu.HBM) for value in (one, two, *held)])
+
+
+def join_kernel(place_ref, w_own, w_other, v, part, *refs):
+    outs, rest = refs[:-1], refs[-1]
+    halves, chips, cores, share = rest.shape[:4]
     lanes = v.shape[4]
-    d0 = place_ref[1]
-    wr, wi = (jnp.concatenate([w_own[r], w_other[r]], axis=1) for r in range(2))
-    for u in range(2):
-        vr = jnp.concatenate([v[d0, 0, u], v[1 - d0, 0, u]], axis=0)
-        vi = jnp.concatenate([v[d0, 1, u], v[1 - d0, 1, u]], axis=0)
-        yr, yi = complex_dot(wr, wi, vr, vi)
-        for r, y in enumerate((yr, yi)):
-            out[:, (2 * r + u) * lanes:(2 * r + u + 1) * lanes] = (part[u, r] + y).astype(BF)
-
-
-def joined(place, weights, v, part):
+    count = chips * cores * share
+    top, core, chip = place_ref[0], place_ref[1], place_ref[2]
+    for h in range(halves):
+        rows = pl.ds(h * count, count)
+        wr, wi = (jnp.concatenate([w_own[r, rows, :], w_other[r, rows, :]], axis=1) for r in range(2))
+        for u in range(2):
+            vr = jnp.concatenate([v[core, 0, u], v[1 - core, 0, u]], axis=0)
+            vi = jnp.concatenate([v[core, 1, u], v[1 - core, 1, u]], axis=0)
+            yr, yi = complex_dot(wr, wi, vr, vi)
+            for r, y in enumerate((yr, yi)):
+                total = (part[u, r, rows, :] + y).astype(BF)
+                columns = pl.ds((2 * r + u) * lanes, lanes)
+                for n in range(chips * cores):
+                    rest[h, n // cores, n % cores, :, columns] = total[n * share:(n + 1) * share]
+    for n, out in enumerate(outs):
+        for e in range(cores):
+            out[e] = rest[1 - top if n < chips else top, chip ^ (n % chips), core ^ e]
+
+
+def joined(groups, place, weights, v, part):
     rows, inner = weights[0].shape[1:]
     lanes = v.shape[4]
-    return pl.pallas_call(
+    outs = pl.pallas_call(
         join_kernel,
         in_specs=[pl.BlockSpec(memory_space=pltpu.SMEM)] + inside(4),
-        out_specs=inside(1)[0],
-        out_shape=jax.ShapeDtypeStruct((rows, 4 * lanes), BF),
+        out_specs=inside(groups // 2),
+        out_shape=[jax.ShapeDtypeStruct((2, rows // groups, 4 * lanes), BF)] * (groups // 2),
+        scratch_shapes=[pltpu.VMEM((2, groups // 4, 2, rows // groups, 4 * lanes), BF)],
         cost_estimate=pl.CostEstimate(flops=32 * rows * inner * lanes, transcendentals=0, bytes_accessed=24 * rows * inner),
         compiler_params=params(16),
         name="join",
     )(place, *weights, v, part)
+    return outs[:groups // 4], outs[groups // 4:]
 
 
 def pick_kernel(own_ref, pick_ref, branch_hbm, out_hbm, held, sem, out_sem):
@@ -213,6 +226,28 @@
     )(own.reshape(1).astype(jnp.int32), slice_pick, branch)
 
 
+def relay_kernel(middle_ref, swapped, chosen, out):
+    @pl.when(middle_ref[0] == 1)
+    def _():
+        out[...] = swapped[...]
+
+    @pl.when(middle_ref[0] == 0)
+    def _():
+        out[...] = chosen[...]
+
+
+def relayed(middle, swapped, chosen):
+    return pl.pallas_call(
+        relay_kernel,
+        in_specs=[pl.BlockSpec(memory_space=pltpu.SMEM)] + inside(2),
+        out_specs=inside(1)[0],
+        out_shape=jax.ShapeDtypeStruct(chosen.shape, BF),
+        cost_estimate=pl.CostEstimate(flops=0, transcendentals=0, bytes_accessed=6 * chosen.size),
+        compiler_params=params(8),
+        name="relay",
+    )(middle.reshape(1).astype(jnp.int32), swapped, chosen)
+
+
 def per_device(stem, branch_one, branch_two, branch_three, leg_orders, slice_pick):
     groups = lax.axis_size("modes")
     own = lax.axis_index("modes")
@@ -247,18 +282,39 @@
         arrived = arrived.transpose(1, 2, 3, 0, 4, 5).reshape(1, 2, 2, 2, side * extent, lanes)
 
     start = (top * (leg_width // 2)).reshape(1).astype(jnp.int32)
-    place = jnp.stack([top, core]).astype(jnp.int32)
+    place = jnp.stack([top, core, own % side // 2]).astype(jnp.int32)
     one = turned(0, start, leg_width // 2, leg_orders, branch_one)
     two = turned(1, jnp.zeros_like(start), leg_width, leg_orders, branch_two)
     swapped, one, two = lax.optimization_barrier((swapped, one, two))
-    other = move(jnp.where(middle, swapped, chosen), cycle)
+    other = move(relayed(middle, swapped, chosen), cycle)
     v, part = chained(place, arrived, one, two, (chosen, near))
     other, v = lax.optimization_barrier((other, v))
     far = move(other, beside)
-    partial = joined(place, (other, far), v, part)
-    spread = lax.all_to_all(partial.reshape(groups, share, 4 * lanes), "modes", 0, 0, tiled=True)
-    total = jnp.sum(spread.reshape(side, 2, share, 4 * lanes).astype(F32), axis=0).astype(BF)
-    return total.reshape(2, share, 2, 2, lanes).transpose(1, 2, 3, 0, 4)
+    weights = (other, far)
+
+    def relative(offset):
+        return [(i, i ^ offset) for i in range(groups)]
+
+    def exchanged(sent):
+        return [move(sent[s], relative(2 * s)) for s in range(1, groups // 4)]
+
+    def added(sent, came):
+        total = sent[0].astype(F32)
+        for piece in came:
+            total = total + piece.astype(F32)
+        return total
+
+    push, pull = joined(groups, place, weights, v, part)
+    pushed = exchanged(push)
+    pulled = exchanged(pull)
+    crossing = added(push, pushed).astype(BF)
+    straight = move(crossing[0], relative(side))
+    slanted = move(crossing[1], relative(side + 1))
+    kept = added(pull, pulled)
+    passed = move(kept[1].astype(BF), beside)
+    mine = (kept[0] + straight.astype(F32)).astype(BF).reshape(share, 2, 2, lanes)
+    yours = (passed.astype(F32) + slanted.astype(F32)).astype(BF).reshape(share, 2, 2, lanes)
+    return jnp.where(core == 0, jnp.stack([mine, yours], axis=3), jnp.stack([yours, mine], axis=3))
 
 
 def solution(mesh):

time: 105 us -> 98.6 us (0.939)
  blocking collectives: 30.8 us -> 0 us
  starting transfers between devices: 20.7 us -> 33.7 us
  waiting for transfers between devices: 3.09 us -> 15.1 us
  local copies, waits for them, and re-layouts: 16 us -> 11.5 us
  Pallas kernels: 33 us -> 35.9 us
    all_to_all x1 -> x0, blocking collectives: 30.8 us -> none  [per_device(): lax.all_to_all(partial.reshape(groups, share, 4 * lanes), 'modes', 0, 0,...]
    ppermute x4 -> x13, starting transfers between devices: 15.3 us -> 28.3 us  [move(): return lax.ppermute(value, 'modes', route)]
    ppermute x4 -> x13, waiting for transfers between devices: 3.09 us -> 15.1 us  [move(): return lax.ppermute(value, 'modes', route)]
    unnamed x20 -> x18, local copies, waits for them, and re-layouts: 12.3 us -> 8.62 us
    pallas_call x0 -> x1, Pallas kernels: none -> 2.29 us  [relayed(): pl.pallas_call(relay_kernel, in_specs=[pl.BlockSpec(memory_space=pltpu.SM...]
  transfers between devices with their start and end apart: 5 -> 14, of which waited for: 2 -> 6; matrix products, arithmetic and copies ran while one was open for 1% -> 0% of each run, Pallas kernels for 27% -> 32%
where the time goes in v3:
time: 98.6 us; the launch traced here: 97.8 us
  Pallas kernels  35.9 us (36%)
  starting transfers between devices  33.7 us (34%)
  waiting for transfers between devices  15.1 us (15%)
  local copies, waits for them, and re-layouts  11.5 us (12%)
  other arithmetic  1.45 us (1%)
    ppermute x13, starting transfers between devices, move(): return lax.ppermute(value, 'modes', route)  28.3 us
    pallas_call x1, Pallas kernels, chained(): pl.pallas_call(chain_kernel, in_specs=[pl.BlockSpec(memory_space=pltpu.SM...  18.2 us
    ppermute x13, waiting for transfers between devices, move(): return lax.ppermute(value, 'modes', route)  15.1 us
    pallas_call x2, Pallas kernels, turned(): pl.pallas_call(lambda *refs: turn_kernel(row, *refs), in_specs=[smem, sme...  11 us
    unnamed x18, local copies, waits for them, and re-layouts  8.62 us
    all_to_all x1, starting transfers between devices, per_device(): lax.all_to_all(pieces, 'modes', 0, 0, tiled=True, axis_index_groups=halves)  5.4 us
    pallas_call x1, Pallas kernels, joined(): pl.pallas_call(join_kernel, in_specs=[pl.BlockSpec(memory_space=pltpu.SME...  3.64 us
    pallas_call x1, Pallas kernels, relayed(): pl.pallas_call(relay_kernel, in_specs=[pl.BlockSpec(memory_space=pltpu.SM...  2.29 us
  transfers between devices with their start and end apart: 14, of which 6 were waited for; matrix products, arithmetic and copies ran while one was open for 0% of the time, Pallas kernels for 32%

profile of v3, /device:TPU:1, one launch (start us, length us, event | category | flops | bytes accessed | tf_op | source)
XLA Modules:
  0.0 97.8 jit_solution(12881361440588878899)
XLA Ops:
  0.0 1.6 %copy-done.1 = bf16[2,2,1,512,512]{4,3,2,1,0:T(8,128)(2,1)S(1)} copy-done((bf16[2,2,1,512,512]{4,3,2,1,0:T(8,128)(2,1)S(1)}, bf16[2,2,1,512,512]{4,3,2,1,0:T(8,128)(2,1)}, u32[]{:S(2)}) %copy-start.1) | copy-done | bytes 2097176
  5.0 1.6 %copy.18 = bf16[2,64,2,8,2,256]{5,1,4,2,0,3:T(8,128)(2,1)} copy(bf16[2,64,2,8,2,256]{5,1,4,3,2,0:T(8,128)(2,1)S(1)} %bitcast.23) | data formatting | bytes 4194304 | tf_op jit(solution)/shard_map/reshape | solution.py:278
  6.7 5.4 %all-to-all-start = ((bf16[8,2,2,2,64,256]{5,4,3,2,1,0:T(8,128)(2,1)}), bf16[8,2,2,2,64,256]{5,4,3,2,1,0:T(8,128)(2,1)S(1)}, u32[]{:S(2)}, u32[]{:S(2)}) async-start(bf16[8,2,2,2,64,256]{5,4,3,2,1,0:T(8,128)(2,1)} %bitcast.22), calls=%async_computation | async-start | bytes 4194304 | tf_op jit(solution)/shard_map/all_to_all | solution.py:280
  12.1 1.6 %collective-permute-start = (bf16[2,512,512]{2,1,0:T(8,128)(2,1)S(1)}, bf16[2,512,512]{2,1,0:T(8,128)(2,1)}, u32[]{:S(2)}, u32[]{:S(2)}) collective-permute-start(bf16[2,512,512]{2,1,0:T(8,128)(2,1)S(1)} %pick.1.chosen.refs_0_), channel_id=1, source_target_pairs={{4,8},{5,9},{6,10},{7,11},{8,4},{9,5},{10,6},{11,7},{20,24},{21,25... | collective-permute-start | bytes 3145736 | tf_op jit(solution)/shard_map/ppermute | solution.py:273
  13.8 2.2 %copy-done.3 = bf16[2,1024,1024]{2,1,0:T(8,128)(2,1)S(1)} copy-done((bf16[2,1024,1024]{2,1,0:T(8,128)(2,1)S(1)}, bf16[2,1024,1024]{2,1,0:T(8,128)(2,1)}, u32[]{:S(2)}) %copy-start.3) | copy-done | bytes 4194328
  16.0 4.3 %turn.2.one_hbm = bf16[2,1024,512]{2,1,0:T(8,128)(2,1)S(1)} custom-call(s32[1]{0:T(128)} %bitcast.5.refs_0_, s32[2,10]{1,0:T(2,128)S(1)} %copy-done.5, bf16[2,1024,1024]{2,1,0:T(8,128)(2,1)S(1)} %copy-done.3), custom_call_target="tpu_custom_call" | custom-call | flops 2147483648 | bytes 4194304 | tf_op jit(solution)/shard_map/turn/pallas_call | solution.py:69
  21.6 6.8 %turn.3.two_hbm = bf16[2,1024,1024]{2,1,0:T(8,128)(2,1)S(1)} custom-call(s32[1]{0:T(128)} %constant.63.clone.1.refs_0_, s32[2,10]{1,0:T(2,128)S(1)} %copy-done.5, bf16[2,1024,1024]{2,1,0:T(8,128)(2,1)S(1)} %copy-done.4), custom_call_target="tpu_custom_call" | custom-call | flops 4294967296 | bytes 4194304 | tf_op jit(solution)/shard_map/turn/pallas_call | solution.py:69
  28.4 1.9 %copy-done.7 = bf16[2,1024,1024]{2,1,0:T(8,128)(2,1)} copy-done((bf16[2,1024,1024]{2,1,0:T(8,128)(2,1)}, bf16[2,1024,1024]{2,1,0:T(8,128)(2,1)S(1)}, u32[]{:S(2)}) %copy-start.7) | copy-done | bytes 4194328
  30.4 2.3 %relay.1 = bf16[2,512,512]{2,1,0:T(8,128)(2,1)} custom-call(s32[1]{0:T(128)} %bitcast.3.middle_ref, bf16[2,512,512]{2,1,0:T(8,128)(2,1)} %collective-permute-done.swapped, bf16[2,512,512]{2,1,0:T(8,128)(2,1)S(1)} %pick.1.chosen.refs_0_), custom_call_target="tpu_custom_call" | custom-call | bytes 3145728 | tf_op jit(solution)/shard_map/relay/pallas_call | solution.py:240
  32.7 10.7 %collective-permute-start.1 = (bf16[2,512,512]{2,1,0:T(8,128)(2,1)}, bf16[2,512,512]{2,1,0:T(8,128)(2,1)}, u32[]{:S(2)}, u32[]{:S(2)}) collective-permute-start(bf16[2,512,512]{2,1,0:T(8,128)(2,1)} %relay.1), channel_id=1, source_target_pairs={{0,8},{1,9},{2,10},{3,11},{8,12},{9,13},{10,14},{11,15},{12,4},{13... | collective-permute-start | bytes 3145736 | tf_op jit(solution)/shard_map/ppermute | solution.py:273
  43.4 18.2 %chain.1 = (bf16[2,2,2,512,256]{4,3,2,1,0:T(8,128)(2,1)S(1)}, f32[2,2,512,256]{3,2,1,0:T(8,128)S(1)}) custom-call(s32[3]{0:T(128)S(1)} %pad_add_fusion.place_ref, bf16[8,2,2,2,64,256]{5,4,3,2,1,0:T(8,128)(2,1)S(1)} %all-to-all-done.x, bf16[2,1024,512]{2,1,0:T(8,128)(2,1)} %copy-done.6, bf16[2,1024,1024]{2,1,0:T(8,128)(2,1)} %copy-done.7, ...), custom_call_target="tpu_custom_call" | custom-call | flops 15032385536 | bytes 18874368 | tf_op jit(solution)/shard_map/chain/pallas_call | solution.py:141
  61.6 3.8 %collective-permute-done.1.w_own = bf16[2,512,512]{2,1,0:T(8,128)(2,1)} collective-permute-done((bf16[2,512,512]{2,1,0:T(8,128)(2,1)}, bf16[2,512,512]{2,1,0:T(8,128)(2,1)}, u32[]{:S(2)}, u32[]{:S(2)}) %collective-permute-start.1) | collective-permute-done | bytes 1048608 | tf_op jit(solution)/shard_map/ppermute | solution.py:273
  65.3 1.7 %collective-permute-start.3 = (bf16[2,512,512]{2,1,0:T(8,128)(2,1)}, bf16[2,512,512]{2,1,0:T(8,128)(2,1)S(1)}, u32[]{:S(2)}, u32[]{:S(2)}) collective-permute-start(bf16[2,512,512]{2,1,0:T(8,128)(2,1)} %collective-permute-done.1.w_own), channel_id=1, source_target_pairs={{0,1},{1,0},{2,3},{3,2},{4,5},{5,4},{6,7},{7,6},{8,9},{9,8},{10,11... | collective-permute-start | bytes 3145736 | tf_op jit(solution)/shard_map/ppermute | solution.py:273
  67.0 2.5 %collective-permute-done.3.w_other = bf16[2,512,512]{2,1,0:T(8,128)(2,1)S(1)} collective-permute-done((bf16[2,512,512]{2,1,0:T(8,128)(2,1)}, bf16[2,512,512]{2,1,0:T(8,128)(2,1)S(1)}, u32[]{:S(2)}, u32[]{:S(2)}) %collective-permute-start.3) | collective-permute-done | bytes 1048608 | tf_op jit(solution)/shard_map/ppermute | solution.py:273
  69.5 3.6 %join.1 = (bf16[2,32,1024]{2,1,0:T(8,128)(2,1)S(1)}, bf16[2,32,1024]{2,1,0:T(8,128)(2,1)S(1)}, bf16[2,32,1024]{2,1,0:T(8,128)(2,1)S(1)}, bf16[2,32,1024]{2,1,0:T...) custom-call(s32[3]{0:T(128)S(1)} %pad_add_fusion.place_ref, ...), custom_call_target="tpu_custom_call" | custom-call | flops 2147483648 | bytes 6291456 | tf_op jit(solution)/shard_map/join/pallas_call | solution.py:185
  74.2 2.0 %collective-permute-start.8 = (bf16[2,32,1024]{2,1,0:T(8,128)(2,1)S(1)}, bf16[2,32,1024]{2,1,0:T(8,128)(2,1)S(1)}, u32[]{:S(2)}, u32[]{:S(2)}) collective-permute-start(bf16[2,32,1024]{2,1,0:T(8,128)(2,1)S(1)} %get-tuple-element.37), channel_id=1, source_target_pairs={{0,4},{1,5},{2,6},{3,7},{4,0},{5,1},{6,2},{7,3},{8,12},{9,13},{10,... | collective-permute-start | bytes 393224 | tf_op jit(solution)/shard_map/ppermute | solution.py:273
  77.4 1.5 %collective-permute-start.5 = (bf16[2,32,1024]{2,1,0:T(8,128)(2,1)S(1)}, bf16[2,32,1024]{2,1,0:T(8,128)(2,1)S(1)}, u32[]{:S(2)}, u32[]{:S(2)}) collective-permute-start(bf16[2,32,1024]{2,1,0:T(8,128)(2,1)S(1)} %get-tuple-element.33), channel_id=1, source_target_pairs={{0,4},{1,5},{2,6},{3,7},{4,0},{5,1},{6,2},{7,3},{8,12},{9,13},{10,... | collective-permute-start | bytes 393224 | tf_op jit(solution)/shard_map/ppermute | solution.py:273
  78.9 1.7 %collective-permute-start.6 = (bf16[2,32,1024]{2,1,0:T(8,128)(2,1)S(1)}, bf16[2,32,1024]{2,1,0:T(8,128)(2,1)S(1)}, u32[]{:S(2)}, u32[]{:S(2)}) collective-permute-start(bf16[2,32,1024]{2,1,0:T(8,128)(2,1)S(1)} %get-tuple-element.34), channel_id=1, source_target_pairs={{0,6},{1,7},{2,4},{3,5},{4,2},{5,3},{6,0},{7,1},{8,14},{9,15},{10,... | collective-permute-start | bytes 393224 | tf_op jit(solution)/shard_map/ppermute | solution.py:273
  80.6 1.6 %collective-permute-done.9 = bf16[2,32,1024]{2,1,0:T(8,128)(2,1)S(1)} collective-permute-done((bf16[2,32,1024]{2,1,0:T(8,128)(2,1)S(1)}, bf16[2,32,1024]{2,1,0:T(8,128)(2,1)S(1)}, u32[]{:S(2)}, u32[]{:S(2)}) %collective-permute-start.9) | collective-permute-done | bytes 131104 | tf_op jit(solution)/shard_map/ppermute | solution.py:273
  82.2 2.7 %collective-permute-start.10 = (bf16[32,1024]{1,0:T(8,128)(2,1)S(1)}, bf16[32,1024]{1,0:T(8,128)(2,1)S(1)}, u32[]{:S(2)}, u32[]{:S(2)}) collective-permute-start(bf16[32,1024]{1,0:T(8,128)(2,1)S(1)} %get-tuple-element.39), channel_id=1, source_target_pairs={{0,8},{1,9},{2,10},{3,11},{4,12},{5,13},{6,14},{7,15},{8,0},{9,1},... | collective-permute-start | bytes 196616 | tf_op jit(solution)/shard_map/ppermute | solution.py:273
  85.1 3.4 %collective-permute-done.6 = bf16[2,32,1024]{2,1,0:T(8,128)(2,1)S(1)} collective-permute-done((bf16[2,32,1024]{2,1,0:T(8,128)(2,1)S(1)}, bf16[2,32,1024]{2,1,0:T(8,128)(2,1)S(1)}, u32[]{:S(2)}, u32[]{:S(2)}) %collective-permute-start.6) | collective-permute-done | bytes 131104 | tf_op jit(solution)/shard_map/ppermute | solution.py:273
  88.6 1.4 %collective-permute-start.11 = (bf16[32,1024]{1,0:T(8,128)(2,1)S(1)}, bf16[32,1024]{1,0:T(8,128)(2,1)S(1)}, u32[]{:S(2)}, u32[]{:S(2)}) collective-permute-start(bf16[32,1024]{1,0:T(8,128)(2,1)S(1)} %fusion.2), channel_id=1, source_target_pairs={{0,1},{1,0},{2,3},{3,2},{4,5},{5,4},{6,7},{7,6},{8,9},{9,8},{10,11... | collective-permute-start | bytes 196616 | tf_op jit(solution)/shard_map/ppermute | solution.py:273
  90.0 2.7 %collective-permute-start.12 = (bf16[32,1024]{1,0:T(8,128)(2,1)S(1)}, bf16[32,1024]{1,0:T(8,128)(2,1)S(1)}, u32[]{:S(2)}, u32[]{:S(2)}) collective-permute-start(bf16[32,1024]{1,0:T(8,128)(2,1)S(1)} %get-tuple-element.40), channel_id=1, source_target_pairs={{0,9},{1,8},{2,11},{3,10},{4,13},{5,12},{6,15},{7,14},{8,1},{9,0},... | collective-permute-start | bytes 196616 | tf_op jit(solution)/shard_map/ppermute | solution.py:273
  92.8 3.7 %collective-permute-done.12 = bf16[32,1024]{1,0:T(8,128)(2,1)S(1)} collective-permute-done((bf16[32,1024]{1,0:T(8,128)(2,1)S(1)}, bf16[32,1024]{1,0:T(8,128)(2,1)S(1)}, u32[]{:S(2)}, u32[]{:S(2)}) %collective-permute-start.12) | collective-permute-done | bytes 65568 | tf_op jit(solution)/shard_map/ppermute | solution.py:273
  (40 shorter events, 8.8 us)
Async XLA Ops:
  0.0 1.6 %copy-start.1 = (bf16[2,2,1,512,512]{4,3,2,1,0:T(8,128)(2,1)S(1)}, bf16[2,2,1,512,512]{4,3,2,1,0:T(8,128)(2,1)}, u32[]{:S(2)}) copy-start(bf16[2,2,1,512,512]{4,3,2,1,0:T(8,128)(2,1)} %branch_hbm.1) | copy-start | bytes 6291460
  1.6 0.7 copy-start.2
  2.2 1.6 %copy-start.8 = (bf16[2,1,64,32,256]{4,3,2,1,0:T(8,128)(2,1)S(1)}, bf16[2,1,64,32,256]{4,3,2,1,0:T(8,128)(2,1)}, u32[]{:S(2)}) copy-start(bf16[2,1,64,32,256]{4,3,2,1,0:T(8,128)(2,1)} %param.6) | copy-start | bytes 6291460
  3.8 26.5 %copy-start = (bf16[2,512,512]{2,1,0:T(8,128)(2,1)}, bf16[2,512,512]{2,1,0:T(8,128)(2,1)S(1)}, u32[]{:S(2)}) copy-start(bf16[2,512,512]{2,1,0:T(8,128)(2,1)S(1)} %pick.1.chosen.refs_0_) | copy-start | bytes 3145732
  6.6 7.1 %copy-start.5 = (s32[2,10]{1,0:T(2,128)S(1)}, s32[2,10]{1,0:T(2,128)}, u32[]{:S(2)}) copy-start(s32[2,10]{1,0:T(2,128)} %refs_1_.3) | copy-start | bytes 244
  6.7 36.7 %all-to-all-start = ((bf16[8,2,2,2,64,256]{5,4,3,2,1,0:T(8,128)(2,1)}), bf16[8,2,2,2,64,256]{5,4,3,2,1,0:T(8,128)(2,1)S(1)}, u32[]{:S(2)}, u32[]{:S(2)}) async-start(bf16[8,2,2,2,64,256]{5,4,3,2,1,0:T(8,128)(2,1)} %bitcast.22), calls=%async_computation | async-start | bytes 4194304 | tf_op jit(solution)/shard_map/all_to_all | solution.py:280
  12.1 18.3 %collective-permute-start = (bf16[2,512,512]{2,1,0:T(8,128)(2,1)S(1)}, bf16[2,512,512]{2,1,0:T(8,128)(2,1)}, u32[]{:S(2)}, u32[]{:S(2)}) collective-permute-start(bf16[2,512,512]{2,1,0:T(8,128)(2,1)S(1)} %pick.1.chosen.refs_0_), channel_id=1, source_target_pairs={{4,8},{5,9},{6,10},{7,11},{8,4},{9,5},{10,6},{11,7},{20,24},{21,25... | collective-permute-start | bytes 3145736 | tf_op jit(solution)/shard_map/ppermute | solution.py:273
  13.7 29.7 %collective-permute-start.2 = (bf16[2,512,512]{2,1,0:T(8,128)(2,1)S(1)}, bf16[2,512,512]{2,1,0:T(8,128)(2,1)}, u32[]{:S(2)}, u32[]{:S(2)}) collective-permute-start(bf16[2,512,512]{2,1,0:T(8,128)(2,1)S(1)} %pick.1.chosen.refs_0_), channel_id=1, source_target_pairs={{0,1},{1,0},{2,3},{3,2},{4,5},{5,4},{6,7},{7,6},{8,9},{9,8},{10,11... | collective-permute-start | bytes 3145736 | tf_op jit(solution)/shard_map/ppermute | solution.py:273
  13.8 2.2 %copy-start.3 = (bf16[2,1024,1024]{2,1,0:T(8,128)(2,1)S(1)}, bf16[2,1024,1024]{2,1,0:T(8,128)(2,1)}, u32[]{:S(2)}) copy-start(bf16[2,1024,1024]{2,1,0:T(8,128)(2,1)} %refs_2_.2) | copy-start | bytes 12582916
  16.0 5.7 %copy-start.4 = (bf16[2,1024,1024]{2,1,0:T(8,128)(2,1)S(1)}, bf16[2,1024,1024]{2,1,0:T(8,128)(2,1)}, u32[]{:S(2)}) copy-start(bf16[2,1024,1024]{2,1,0:T(8,128)(2,1)} %refs_2_.3) | copy-start | bytes 12582916
  20.2 1.4 %copy-start.6 = (bf16[2,1024,512]{2,1,0:T(8,128)(2,1)}, bf16[2,1024,512]{2,1,0:T(8,128)(2,1)S(1)}, u32[]{:S(2)}) copy-start(bf16[2,1024,512]{2,1,0:T(8,128)(2,1)S(1)} %turn.2.one_hbm) | copy-start | bytes 6291460
  28.4 1.9 %copy-start.7 = (bf16[2,1024,1024]{2,1,0:T(8,128)(2,1)}, bf16[2,1024,1024]{2,1,0:T(8,128)(2,1)S(1)}, u32[]{:S(2)}) copy-start(bf16[2,1024,1024]{2,1,0:T(8,128)(2,1)S(1)} %turn.3.two_hbm) | copy-start | bytes 12582916
  32.7 32.7 %collective-permute-start.1 = (bf16[2,512,512]{2,1,0:T(8,128)(2,1)}, bf16[2,512,512]{2,1,0:T(8,128)(2,1)}, u32[]{:S(2)}, u32[]{:S(2)}) collective-permute-start(bf16[2,512,512]{2,1,0:T(8,128)(2,1)} %relay.1), channel_id=1, source_target_pairs={{0,8},{1,9},{2,10},{3,11},{8,12},{9,13},{10,14},{11,15},{12,4},{13... | collective-permute-start | bytes 3145736 | tf_op jit(solution)/shard_map/ppermute | solution.py:273
  65.3 4.2 %collective-permute-start.3 = (bf16[2,512,512]{2,1,0:T(8,128)(2,1)}, bf16[2,512,512]{2,1,0:T(8,128)(2,1)S(1)}, u32[]{:S(2)}, u32[]{:S(2)}) collective-permute-start(bf16[2,512,512]{2,1,0:T(8,128)(2,1)} %collective-permute-done.1.w_own), channel_id=1, source_target_pairs={{0,1},{1,0},{2,3},{3,2},{4,5},{5,4},{6,7},{7,6},{8,9},{9,8},{10,11... | collective-permute-start | bytes 3145736 | tf_op jit(solution)/shard_map/ppermute | solution.py:273
  73.2 5.7 %collective-permute-start.7 = (bf16[2,32,1024]{2,1,0:T(8,128)(2,1)S(1)}, bf16[2,32,1024]{2,1,0:T(8,128)(2,1)S(1)}, u32[]{:S(2)}, u32[]{:S(2)}) collective-permute-start(bf16[2,32,1024]{2,1,0:T(8,128)(2,1)S(1)} %get-tuple-element.36), channel_id=1, source_target_pairs={{0,2},{1,3},{2,0},{3,1},{4,6},{5,7},{6,4},{7,5},{8,10},{9,11},{10,... | collective-permute-start | bytes 393224 | tf_op jit(solution)/shard_map/ppermute | solution.py:273
  74.2 6.4 %collective-permute-start.8 = (bf16[2,32,1024]{2,1,0:T(8,128)(2,1)S(1)}, bf16[2,32,1024]{2,1,0:T(8,128)(2,1)S(1)}, u32[]{:S(2)}, u32[]{:S(2)}) collective-permute-start(bf16[2,32,1024]{2,1,0:T(8,128)(2,1)S(1)} %get-tuple-element.37), channel_id=1, source_target_pairs={{0,4},{1,5},{2,6},{3,7},{4,0},{5,1},{6,2},{7,3},{8,12},{9,13},{10,... | collective-permute-start | bytes 393224 | tf_op jit(solution)/shard_map/ppermute | solution.py:273
  76.2 6.0 %collective-permute-start.9 = (bf16[2,32,1024]{2,1,0:T(8,128)(2,1)S(1)}, bf16[2,32,1024]{2,1,0:T(8,128)(2,1)S(1)}, u32[]{:S(2)}, u32[]{:S(2)}) collective-permute-start(bf16[2,32,1024]{2,1,0:T(8,128)(2,1)S(1)} %get-tuple-element.38), channel_id=1, source_target_pairs={{0,6},{1,7},{2,4},{3,5},{4,2},{5,3},{6,0},{7,1},{8,14},{9,15},{10,... | collective-permute-start | bytes 393224 | tf_op jit(solution)/shard_map/ppermute | solution.py:273
  76.2 8.7 %collective-permute-start.4 = (bf16[2,32,1024]{2,1,0:T(8,128)(2,1)S(1)}, bf16[2,32,1024]{2,1,0:T(8,128)(2,1)S(1)}, u32[]{:S(2)}, u32[]{:S(2)}) collective-permute-start(bf16[2,32,1024]{2,1,0:T(8,128)(2,1)S(1)} %get-tuple-element.32), channel_id=1, source_target_pairs={{0,2},{1,3},{2,0},{3,1},{4,6},{5,7},{6,4},{7,5},{8,10},{9,11},{10,... | collective-permute-start | bytes 393224 | tf_op jit(solution)/shard_map/ppermute | solution.py:273
  77.4 7.7 %collective-permute-start.5 = (bf16[2,32,1024]{2,1,0:T(8,128)(2,1)S(1)}, bf16[2,32,1024]{2,1,0:T(8,128)(2,1)S(1)}, u32[]{:S(2)}, u32[]{:S(2)}) collective-permute-start(bf16[2,32,1024]{2,1,0:T(8,128)(2,1)S(1)} %get-tuple-element.33), channel_id=1, source_target_pairs={{0,4},{1,5},{2,6},{3,7},{4,0},{5,1},{6,2},{7,3},{8,12},{9,13},{10,... | collective-permute-start | bytes 393224 | tf_op jit(solution)/shard_map/ppermute | solution.py:273
  78.9 9.6 %collective-permute-start.6 = (bf16[2,32,1024]{2,1,0:T(8,128)(2,1)S(1)}, bf16[2,32,1024]{2,1,0:T(8,128)(2,1)S(1)}, u32[]{:S(2)}, u32[]{:S(2)}) collective-permute-start(bf16[2,32,1024]{2,1,0:T(8,128)(2,1)S(1)} %get-tuple-element.34), channel_id=1, source_target_pairs={{0,6},{1,7},{2,4},{3,5},{4,2},{5,3},{6,0},{7,1},{8,14},{9,15},{10,... | collective-permute-start | bytes 393224 | tf_op jit(solution)/shard_map/ppermute | solution.py:273
  82.2 10.5 %collective-permute-start.10 = (bf16[32,1024]{1,0:T(8,128)(2,1)S(1)}, bf16[32,1024]{1,0:T(8,128)(2,1)S(1)}, u32[]{:S(2)}, u32[]{:S(2)}) collective-permute-start(bf16[32,1024]{1,0:T(8,128)(2,1)S(1)} %get-tuple-element.39), channel_id=1, source_target_pairs={{0,8},{1,9},{2,10},{3,11},{4,12},{5,13},{6,14},{7,15},{8,0},{9,1},... | collective-permute-start | bytes 196616 | tf_op jit(solution)/shard_map/ppermute | solution.py:273
  88.6 4.2 %collective-permute-start.11 = (bf16[32,1024]{1,0:T(8,128)(2,1)S(1)}, bf16[32,1024]{1,0:T(8,128)(2,1)S(1)}, u32[]{:S(2)}, u32[]{:S(2)}) collective-permute-start(bf16[32,1024]{1,0:T(8,128)(2,1)S(1)} %fusion.2), channel_id=1, source_target_pairs={{0,1},{1,0},{2,3},{3,2},{4,5},{5,4},{6,7},{7,6},{8,9},{9,8},{10,11... | collective-permute-start | bytes 196616 | tf_op jit(solution)/shard_map/ppermute | solution.py:273
  90.0 6.6 %collective-permute-start.12 = (bf16[32,1024]{1,0:T(8,128)(2,1)S(1)}, bf16[32,1024]{1,0:T(8,128)(2,1)S(1)}, u32[]{:S(2)}, u32[]{:S(2)}) collective-permute-start(bf16[32,1024]{1,0:T(8,128)(2,1)S(1)} %get-tuple-element.40), channel_id=1, source_target_pairs={{0,9},{1,8},{2,11},{3,10},{4,13},{5,12},{6,15},{7,14},{8,1},{9,0},... | collective-permute-start | bytes 196616 | tf_op jit(solution)/shard_map/ppermute | solution.py:273
